TPU v7x, 8 devices: a whole 2x2x1 slice. The times are simulated.
8 devices in a mesh: dp: 1 (over z), ch: 2 (over y), wd: 4 (over x, core).
Axes of the slice: x: 2, y: 2, z: 1, core: 2. Of those that a mesh axis runs over, the one named last changes fastest.
Arguments:
- resid_in: bfloat16 [8192, 4096], P('dp', 'wd')
- seg_pos: int32 [2, 4096], P('dp')
- gain_temporal: bfloat16 [4096], P('wd')
- w_x: bfloat16 [4096, 5632], P('wd', 'ch')
- bias_x: bfloat16 [5632], P('ch')
- w_y: bfloat16 [4096, 5632], P('wd', 'ch')
- bias_y: bfloat16 [5632], P('ch')
- conv_w: bfloat16 [4, 5632], P(None, 'ch')
- conv_bias: bfloat16 [5632], P('ch')
- lam_param: float32 [5632], P('ch')
- rgate_w: bfloat16 [22, 256, 256], P('ch')
- rgate_b: bfloat16 [5632], P('ch')
- igate_w: bfloat16 [22, 256, 256], P('ch')
- igate_b: bfloat16 [5632], P('ch')
- w_o: bfloat16 [5632, 4096], P('ch', 'wd')
- bias_o: bfloat16 [4096], P('wd')
- gain_mlp: bfloat16 [4096], P('wd')
- w_g: bfloat16 [4096, 12288], P('wd', 'ch')
- bias_g: bfloat16 [12288], P('ch')
- w_u: bfloat16 [4096, 12288], P('wd', 'ch')
- bias_u: bfloat16 [12288], P('ch')
- w_d: bfloat16 [12288, 4096], P('ch', 'wd')
- bias_d: bfloat16 [4096], P('wd')
Outputs:
- output: bfloat16 [8192, 4096], P('dp', 'wd')
All inputs are finite; a program needn't handle non-finite values.
Results may differ from a plain program's by a relative error of at most 0.0130632.
Values are sent between devices in bfloat16 or wider.
A program may use at most 1 GiB of HBM per device.

v0:
```python
import jax
import jax.numpy as jnp
from jax import lax
from jax.sharding import PartitionSpec as P, NamedSharding

EPS = 1e-6


def rms_apply(vals, sum_sq, width, gain):
    return (vals * lax.rsqrt(sum_sq / width + EPS) * (1.0 + gain.astype(jnp.float32))).astype(jnp.bfloat16)


def token_sum(part_sum, axis_name, count):
    tokens, width = part_sum.shape
    pieces = part_sum.astype(jnp.bfloat16).reshape(count, tokens // count, width)
    received = lax.all_to_all(pieces, axis_name, 0, 0)
    return jnp.sum(received.astype(jnp.float32), axis=0)


def conv_mix(vals, positions, conv_w, conv_bias):
    vals32 = vals.astype(jnp.float32)
    taps = conv_w.astype(jnp.float32)
    total = conv_bias.astype(jnp.float32) + vals32 * taps[0]
    for shift in range(1, conv_w.shape[0]):
        moved = jnp.pad(vals32[:-shift], ((shift, 0), (0, 0)))
        total = total + jnp.where((positions >= shift)[:, None], moved, 0.0) * taps[shift]
    return total.astype(jnp.bfloat16)


def combine(left, right):
    return left[0] * right[0], right[0] * left[1] + right[1]


def rg_lru(conv_out, positions, seqs, lam_param, rgate_w, rgate_b, igate_w, igate_b):
    tokens, width = conv_out.shape
    blocks = rgate_w.shape[0]
    grouped = conv_out.reshape(tokens, blocks, width // blocks)
    rate = jax.nn.sigmoid(jnp.einsum('nbi,bij->nbj', grouped, rgate_w, preferred_element_type=jnp.float32).reshape(tokens, width) + rgate_b.astype(jnp.float32))
    inflow = jax.nn.sigmoid(jnp.einsum('nbi,bij->nbj', grouped, igate_w, preferred_element_type=jnp.float32).reshape(tokens, width) + igate_b.astype(jnp.float32))
    log_a = -8.0 * rate * jax.nn.softplus(-lam_param)
    reset = (positions == 0)[:, None]
    decay = jnp.where(reset, 0.0, jnp.exp(log_a))
    scale = jnp.where(reset, 1.0, jnp.sqrt(-jnp.expm1(2.0 * log_a)))
    drive = scale * inflow * conv_out.astype(jnp.float32)
    steps = tokens // seqs
    hidden = lax.associative_scan(combine, (decay.reshape(seqs, steps, width), drive.reshape(seqs, steps, width)), axis=1)[1]
    return hidden.reshape(tokens, width)


def solution(mesh):
    wd_count = mesh.shape['wd']
    ch_count = mesh.shape['ch']
    row_spec = P('dp', 'wd')
    specs = (row_spec, P('dp', None), P('wd'), P('wd', 'ch'), P('ch'), P('wd', 'ch'), P('ch'), P(None, 'ch'), P('ch'), P('ch'), P('ch', None, None), P('ch'), P('ch', None, None), P('ch'), P('ch', 'wd'), P('wd'), P('wd'), P('wd', 'ch'), P('ch'), P('wd', 'ch'), P('ch'), P('ch', 'wd'), P('wd'))

    def local_layer(resid_in, seg_pos, gain_temporal, w_x, bias_x, w_y, bias_y, conv_w, conv_bias, lam_param, rgate_w, rgate_b, igate_w, igate_b, w_o, bias_o, gain_mlp, w_g, bias_g, w_u, bias_u, w_d, bias_d):
        tokens, local_width = resid_in.shape
        model_width = local_width * wd_count
        share = tokens // ch_count
        positions = seg_pos.reshape(tokens)
        resid32 = resid_in.astype(jnp.float32)
        sum_sq = lax.psum(jnp.sum(resid32 * resid32, axis=1, keepdims=True), 'wd')
        normed = rms_apply(resid32, sum_sq, model_width, gain_temporal)
        y_sum = token_sum(jnp.dot(normed, w_y, preferred_element_type=jnp.float32), 'wd', wd_count)
        y_rows = jax.nn.gelu(y_sum + bias_y.astype(jnp.float32), approximate=True).astype(jnp.bfloat16)
        y_branch = lax.all_gather(y_rows, 'wd', axis=0, tiled=True)
        u_sum = token_sum(jnp.dot(normed, w_x, preferred_element_type=jnp.float32), 'wd', wd_count)
        u_rows = (u_sum + bias_x.astype(jnp.float32)).astype(jnp.bfloat16)
        u_branch = lax.all_gather(u_rows, 'wd', axis=0, tiled=True)
        conv_out = conv_mix(u_branch, positions, conv_w, conv_bias)
        hidden = rg_lru(conv_out, positions, seg_pos.shape[0], lam_param, rgate_w, rgate_b, igate_w, igate_b)
        mixed = (hidden * y_branch.astype(jnp.float32)).astype(jnp.bfloat16)
        mix_sum = token_sum(jnp.dot(mixed, w_o, preferred_element_type=jnp.float32), 'ch', ch_count)
        resid_rows = lax.dynamic_slice_in_dim(resid32, lax.axis_index('ch') * share, share, axis=0)
        resid = resid_rows + mix_sum + bias_o.astype(jnp.float32)
        sum_sq2 = lax.psum(jnp.sum(resid * resid, axis=1, keepdims=True), 'wd')
        normed2 = lax.all_gather(rms_apply(resid, sum_sq2, model_width, gain_mlp), 'ch', axis=0, tiled=True)
        gate_sum = token_sum(jnp.dot(normed2, w_g, preferred_element_type=jnp.float32), 'wd', wd_count)
        up_sum = token_sum(jnp.dot(normed2, w_u, preferred_element_type=jnp.float32), 'wd', wd_count)
        inner_rows = (jax.nn.gelu(gate_sum + bias_g.astype(jnp.float32), approximate=True) * (up_sum + bias_u.astype(jnp.float32))).astype(jnp.bfloat16)
        inner = lax.all_gather(inner_rows, 'wd', axis=0, tiled=True)
        down_sum = token_sum(jnp.dot(inner, w_d, preferred_element_type=jnp.float32), 'ch', ch_count)
        out_rows = (resid + down_sum + bias_d.astype(jnp.float32)).astype(jnp.bfloat16)
        return lax.all_gather(out_rows, 'ch', axis=0, tiled=True)

    return jax.shard_map(local_layer, mesh=mesh, in_specs=specs, out_specs=row_spec, check_vma=False)
```

profile of v0, /device:TPU:0, one launch (start us, length us, event | category | flops | bytes accessed | tf_op | source)
XLA Modules:
  0.0 9644.5 jit_solution(5238299013216616472)
XLA Ops:
  27.9 58.2 convolution_convert_fusion.3
  98.0 497.0 %all-to-all-done = bf16[4,2048,2816]{2,1,0:T(8,128)(2,1)} async-done(((bf16[4,2048,2816]{2,1,0:T(8,128)(2,1)}), bf16[4,2048,2816]{2,1,0:T(8,128)(2,1)}, u32[]{:S(2)}, u32[]{:S(2)}) %all-to-all-start) | async-done | bytes 46137376 | tf_op jit(solution)/shard_map/all_to_all | solution.py:16
  595.0 33.1 convert_reduce_fusion.3
  640.6 58.2 convolution_convert_fusion.2
  716.7 686.3 %all-to-all-done.1 = bf16[4,2048,2816]{2,1,0:T(8,128)(2,1)} async-done(((bf16[4,2048,2816]{2,1,0:T(8,128)(2,1)}), bf16[4,2048,2816]{2,1,0:T(8,128)(2,1)}, u32[]{:S(2)}, u32[]{:S(2)}) %all-to-all-start.1) | async-done | bytes 46137376 | tf_op jit(solution)/shard_map/all_to_all | solution.py:16
  1403.0 33.1 convert_reduce_fusion.2
  1451.9 44.8 slice.403
  1496.7 44.6 slice.401
  1541.3 45.1 slice.399
  1586.5 132.1 %add_convert_fusion = bf16[8192,2816]{1,0:T(8,128)(2,1)} fusion(f32[8189,2816]{1,0:T(8,128)} %slice.403, f32[8190,2816]{1,0:T(8,128)} %slice.401, f32[8191,2816]{1,0:T(8,128)} %slice.399, f32[2816]{0:T(1024)S(1)} %copy-done.29, f32[2816]{0:T(1024)S(1)} %copy-done.30, f32[2816]{0:T(1024)S(1)} %copy-done.31, f32[2816]{0:T(1024)S(1)} %copy-done.28, ...), kind=kLoop, calls=%fused_computation.7 | loop fusion | flops 299892736 | bytes 369112064 | tf_op jit(solution)/shard_map/convert_element_type | solution.py:27
  1718.6 56.0 copy.30
  1774.6 46.6 fusion.44
  1821.2 114.7 %reshape.96 = f32[2,4096,2816]{1,0,2:T(2,128)} reshape(f32[8192,11,256]{0,2,1:T(8,128)} %bitcast.4) | data formatting | bytes 184549376 | tf_op jit(solution)/shard_map/reshape | solution.py:38
  1935.9 131.1 %copy.37 = f32[2,4096,2816]{2,1,0:T(8,128)} copy(f32[2,4096,2816]{1,0,2:T(2,128)} %reshape.96) | data formatting | bytes 184549376 | tf_op jit(solution)/shard_map/reshape | solution.py:38
  2067.0 61.2 exponential_select_fusion
  2128.2 151.9 %slice.308 = f32[2,2047,2816]{2,1,0:T(8,128)} slice(f32[2,4096,2816]{2,1,0:T(8,128)} %exponential_select_fusion), slice={[0:2:1], [2:4096:2], [0:2816:1]} | slice | bytes 92229632 | tf_op jit(solution)/shard_map/slice | solution.py:46
  2280.1 146.8 %slice.313 = f32[2,2048,2816]{2,1,0:T(8,128)} slice(f32[2,4096,2816]{2,1,0:T(8,128)} %exponential_select_fusion), slice={[0:2:1], [0:4095:2], [0:2816:1]} | slice | bytes 92274688 | tf_op jit(solution)/shard_map/slice | solution.py:46
  2426.8 146.8 %slice.309 = f32[2,2048,2816]{2,1,0:T(8,128)} slice(f32[2,4096,2816]{2,1,0:T(8,128)} %exponential_select_fusion), slice={[0:2:1], [1:4096:2], [0:2816:1]} | slice | bytes 92274688 | tf_op jit(solution)/shard_map/slice | solution.py:46
  2573.6 46.6 fusion.45
  2620.2 91.7 copy.36
  2712.0 91.7 copy.33
  2803.7 119.7 %convert_multiply_fusion = f32[8192,2816]{1,0:T(8,128)} fusion(bf16[8192,2816]{1,0:T(8,128)(2,1)} %add_convert_fusion, f32[8192,2816]{1,0:T(8,128)} %copy.36, f32[8192,2816]{1,0:T(8,128)} %copy.33, f32[2816]{0:T(1024)S(1)} %copy-done.26, f32[2816]{0:T(1024)S(1)} %copy-done.18, f32[2816]{0:T(1024)S(1)} %copy-done.16, pred[8192]{0:T(1024)(128)(4,1)S(1)} %copy-done.32), kind=kLoop, calls=%fused_computation.6 | loop fusion | flops 346030080 | bytes 323003392 | tf_op jit(solution)/shard_map/mul | solution.py:44
  2923.4 151.8 %slice.397 = f32[2,2047,2816]{2,1,0:T(8,128)} slice(f32[2,4096,2816]{2,1,0:T(8,128)} %bitcast.8), slice={[0:2:1], [2:4096:2], [0:2816:1]} | slice | bytes 92229632 | tf_op jit(solution)/shard_map/slice | solution.py:46
  3075.2 146.6 %slice.311 = f32[2,2048,2816]{2,1,0:T(8,128)} slice(f32[2,4096,2816]{2,1,0:T(8,128)} %bitcast.8), slice={[0:2:1], [1:4096:2], [0:2816:1]} | slice | bytes 92274688 | tf_op jit(solution)/shard_map/slice | solution.py:46
  3221.8 146.7 %slice.310 = f32[2,2048,2816]{2,1,0:T(8,128)} slice(f32[2,4096,2816]{2,1,0:T(8,128)} %bitcast.8), slice={[0:2:1], [0:4095:2], [0:2816:1]} | slice | bytes 92274688 | tf_op jit(solution)/shard_map/slice | solution.py:46
  3368.4 88.0 fusion.32
  3456.4 73.9 slice.319
  3530.3 73.9 slice.315
  3604.2 73.8 slice.317
  3677.9 73.9 slice.316
  3751.9 45.5 fusion.33
  3797.4 38.9 slice.320
  3836.3 37.5 slice.325
  3873.7 37.5 slice.321
  3911.2 38.8 slice.393
  3950.0 37.5 slice.323
  3987.5 37.5 slice.322
  4334.0 76.5 slice.395
  4410.6 76.6 slice.314
  4658.2 43.0 pad.106
  4701.2 42.8 pad.107
  4767.7 85.2 pad.109
  4852.9 37.3 fusion.19
  4906.9 85.1 pad.108
  4991.9 45.6 add.360
  5037.5 72.9 fusion.10
  5143.2 169.7 %pad.110 = f32[2,4096,2816]{2,1,0:T(8,128)} pad(f32[2,2048,2816]{2,1,0:T(8,128)} %pad_maximum_fusion, f32[]{:T(128)} %constant.23.clone.1), padding=0_0_0x0_1_1x0_0_0 | pad | bytes 138412032 | tf_op jit(solution)/shard_map/pad | solution.py:46
  5312.9 170.1 %pad.111 = f32[2,4096,2816]{2,1,0:T(8,128)} pad(f32[2,2048,2816]{2,1,0:T(8,128)} %add.360, f32[]{:T(128)} %constant.23.clone.1), padding=0_0_0x1_0_1x0_0_0 | pad | bytes 138412032 | tf_op jit(solution)/shard_map/pad | solution.py:46
  5483.0 88.9 add.362
  5571.9 58.8 fusion
  5630.7 54.6 convolution_convert_fusion.5
  5713.9 163.5 %all-to-all-done.2 = bf16[2,4096,1024]{2,1,0:T(8,128)(2,1)} async-done(((bf16[2,4096,1024]{2,1,0:T(8,128)(2,1)}), bf16[2,4096,1024]{2,1,0:T(8,128)(2,1)}, u32[]{:S(2)}, u32[]{:S(2)}) %all-to-all-start.2) | async-done | bytes 16777248 | tf_op jit(solution)/shard_map/all_to_all | solution.py:16
  5919.6 196.1 %all-gather.10.cloned.1.call-done = bf16[8192,1024]{1,0:T(8,128)(2,1)} async-done(((bf16[4096,1024]{1,0:T(8,128)(2,1)}), bf16[8192,1024]{1,0:T(8,128)(2,1)}) %all-gather.10.cloned.1.call-update) | async-done | bytes 16777232 | tf_op jit(solution)/shard_map/all_gather | solution.py:77
  6115.8 115.1 %convolution_convert_fusion = bf16[8192,6144]{1,0:T(8,128)(2,1)} fusion(bf16[8192,1024]{1,0:T(8,128)(2,1)} %all-gather.10.cloned.1.call-done, bf16[1024,6144]{1,0:T(8,128)(2,1)} %param.42), kind=kOutput, calls=%fused_computation.9 | convolution fusion | flops 103129546752 | bytes 130023424 | tf_op jit(solution)/shard_map/dot_general | solution.py:79
  6249.8 115.1 %convolution_convert_fusion.1 = bf16[8192,6144]{1,0:T(8,128)(2,1)} fusion(bf16[8192,1024]{1,0:T(8,128)(2,1)} %all-gather.10.cloned.1.call-done, bf16[1024,6144]{1,0:T(8,128)(2,1)} %param.40), kind=kOutput, calls=%fused_computation.10 | convolution fusion | flops 103129546752 | bytes 130023424 | tf_op jit(solution)/shard_map/dot_general | solution.py:78
  6364.9 966.4 %all-to-all-done.4 = bf16[4,2048,6144]{2,1,0:T(8,128)(2,1)} async-done(((bf16[4,2048,6144]{2,1,0:T(8,128)(2,1)}), bf16[4,2048,6144]{2,1,0:T(8,128)(2,1)}, u32[]{:S(2)}, u32[]{:S(2)}) %all-to-all-start.4) | async-done | bytes 100663328 | tf_op jit(solution)/shard_map/all_to_all | solution.py:16
  7350.3 48.1 convert_reduce_fusion
  7398.5 1033.3 %all-to-all-done.3 = bf16[4,2048,6144]{2,1,0:T(8,128)(2,1)} async-done(((bf16[4,2048,6144]{2,1,0:T(8,128)(2,1)}), bf16[4,2048,6144]{2,1,0:T(8,128)(2,1)}, u32[]{:S(2)}, u32[]{:S(2)}) %all-to-all-start.3) | async-done | bytes 100663328 | tf_op jit(solution)/shard_map/all_to_all | solution.py:16
  8431.8 47.9 convert_reduce_fusion.1
  8479.6 40.8 fusion.9
  8520.5 579.1 %all-gather.12.cloned.1.call-done = bf16[8192,6144]{1,0:T(8,128)(2,1)} async-done(((bf16[2048,6144]{1,0:T(8,128)(2,1)}), bf16[8192,6144]{1,0:T(8,128)(2,1)}) %all-gather.12.cloned.1.call-update) | async-done | bytes 100663312 | tf_op jit(solution)/shard_map/all_gather | solution.py:81
  9099.6 114.5 %convolution_convert_fusion.4 = bf16[8192,1024]{1,0:T(8,128)(2,1)} fusion(bf16[8192,6144]{1,0:T(8,128)(2,1)} %all-gather.12.cloned.1.call-done, bf16[6144,1024]{1,0:T(8,128)(2,1)} %param.44), kind=kOutput, calls=%fused_computation.49 | convolution fusion | flops 103087603712 | bytes 130023424 | tf_op jit(solution)/shard_map/dot_general | solution.py:82
  9224.3 182.2 %all-to-all-done.5 = bf16[2,4096,1024]{2,1,0:T(8,128)(2,1)} async-done(((bf16[2,4096,1024]{2,1,0:T(8,128)(2,1)}), bf16[2,4096,1024]{2,1,0:T(8,128)(2,1)}, u32[]{:S(2)}, u32[]{:S(2)}) %all-to-all-start.5) | async-done | bytes 16777248 | tf_op jit(solution)/shard_map/all_to_all | solution.py:16
  9427.9 195.7 %all-gather.14.cloned.1.call-done = bf16[8192,1024]{1,0:T(8,128)(2,1)} async-done(((bf16[4096,1024]{1,0:T(8,128)(2,1)}), bf16[8192,1024]{1,0:T(8,128)(2,1)}) %all-gather.14.cloned.1.call-update) | async-done | bytes 16777232 | tf_op jit(solution)/shard_map/all_gather | solution.py:84
  (261 shorter events, 786.4 us)
Async XLA Ops:
  6.5 1768.1 %copy-start = (bf16[11,256,256]{2,1,0:T(8,128)(2,1)S(1)}, bf16[11,256,256]{2,1,0:T(8,128)(2,1)}, u32[]{:S(2)}) copy-start(bf16[11,256,256]{2,1,0:T(8,128)(2,1)} %param.33) | copy-start | bytes 4325380
  86.0 11.9 copy-start.41
  86.0 509.0 %all-to-all-start = ((bf16[4,2048,2816]{2,1,0:T(8,128)(2,1)}), bf16[4,2048,2816]{2,1,0:T(8,128)(2,1)}, u32[]{:S(2)}, u32[]{:S(2)}) async-start(bf16[4,2048,2816]{2,1,0:T(8,128)(2,1)} %bitcast.48), calls=%async_computation | async-start | bytes 92274688 | tf_op jit(solution)/shard_map/all_to_all | solution.py:16
  97.7 1354.2 %all-gather.6.cloned.1.call-start = ((), (), s32[]{:S(2)}) async-start(), calls=%async_computation.6 | async-start | bytes 57671680 | tf_op jit(solution)/shard_map/all_gather | solution.py:69
  698.7 12.2 copy-start.37
  698.7 12.2 copy-start.42
  698.7 12.8 copy-start.36
  698.7 14.8 copy-start.43
  698.7 15.4 copy-start.44
  698.8 16.6 copy-start.45
  698.8 17.3 copy-start.38
  698.8 704.2 %all-to-all-start.1 = ((bf16[4,2048,2816]{2,1,0:T(8,128)(2,1)}), bf16[4,2048,2816]{2,1,0:T(8,128)(2,1)}, u32[]{:S(2)}, u32[]{:S(2)}) async-start(bf16[4,2048,2816]{2,1,0:T(8,128)(2,1)} %bitcast.47), calls=%async_computation.1 | async-start | bytes 92274688 | tf_op jit(solution)/shard_map/all_to_all | solution.py:16
  710.5 4861.4 %all-gather.8.cloned.1.call-start = ((), (), s32[]{:S(2)}) async-start(), calls=%async_computation.7 | async-start | bytes 57671680 | tf_op jit(solution)/shard_map/all_gather | solution.py:66
  711.6 724.5 %copy-start.13 = (pred[2,4096]{1,0:T(4,128)(4,1)}, pred[2,4096]{1,0:T(4,128)(4,1)S(1)}, u32[]{:S(2)}) copy-start(pred[2,4096]{1,0:T(4,128)(4,1)S(1)} %get-tuple-element.35) | copy-start | bytes 24580
  1541.2 45.2 copy-start.27
  1541.2 45.2 copy-start.28
  1541.2 45.2 copy-start.29
  1541.3 45.2 copy-start.30
  1541.3 45.2 copy-start.31
  1541.3 45.2 copy-start.33
  1541.3 45.2 copy-start.34
  1541.3 45.2 copy-start.35
  1935.9 131.1 %copy-start.14 = (pred[2,4096]{1,0:T(4,128)(4,1)S(1)}, pred[2,4096]{1,0:T(4,128)(4,1)}, u32[]{:S(2)}) copy-start(pred[2,4096]{1,0:T(4,128)(4,1)} %copy-done.13) | copy-start | bytes 24580
  1935.9 131.1 %copy-start.15 = (f32[2816]{0:T(1024)S(1)}, f32[2816]{0:T(1024)}, u32[]{:S(2)}) copy-start(f32[2816]{0:T(1024)} %convert_element_type.125) | copy-start | bytes 33796
  1935.9 131.1 %copy-start.17 = (f32[2816]{0:T(1024)S(1)}, f32[2816]{0:T(1024)}, u32[]{:S(2)}) copy-start(f32[2816]{0:T(1024)} %fusion.31) | copy-start | bytes 33796
  2426.8 146.8 %copy-start.5 = (bf16[11,256,256]{2,1,0:T(8,128)(2,1)S(1)}, bf16[11,256,256]{2,1,0:T(8,128)(2,1)}, u32[]{:S(2)}) copy-start(bf16[11,256,256]{2,1,0:T(8,128)(2,1)} %param.35) | copy-start | bytes 4325380
  2711.9 91.7 copy-start.16
  2711.9 91.7 copy-start.18
  2712.0 91.7 copy-start.26
  2712.0 91.7 copy-start.32
  4410.5 79.7 copy-start.10
  4410.5 79.7 copy-start.11
  4410.5 79.7 copy-start.12
  4410.5 79.8 copy-start.19
  4410.5 81.2 copy-start.8
  4410.5 81.2 copy-start.9
  4410.6 81.3 copy-start.24
  4410.6 81.4 copy-start.6
  4410.6 81.4 copy-start.7
  4410.6 81.5 copy-start.25
  4410.6 86.5 copy-start.3
  4410.6 86.5 copy-start.4
  4499.7 24.2 copy-start.23
  4555.9 33.5 copy-start.22
  4616.9 15.1 copy-start.2
  4852.9 37.3 copy-start.21
  5037.5 72.9 copy-start.20
  5685.3 192.1 %all-to-all-start.2 = ((bf16[2,4096,1024]{2,1,0:T(8,128)(2,1)}), bf16[2,4096,1024]{2,1,0:T(8,128)(2,1)}, u32[]{:S(2)}, u32[]{:S(2)}) async-start(bf16[2,4096,1024]{2,1,0:T(8,128)(2,1)} %bitcast.49), calls=%async_computation.2 | async-start | bytes 33554432 | tf_op jit(solution)/shard_map/all_to_all | solution.py:16
  5695.0 18.9 copy-start.46
  5695.0 18.8 copy-start.47
  5695.0 420.7 %all-gather.10.cloned.1.call-start = ((), (), s32[]{:S(2)}) async-start(), calls=%async_computation.8 | async-start | bytes 25165824 | tf_op jit(solution)/shard_map/all_gather | solution.py:77
  6230.9 1100.5 %all-to-all-start.4 = ((bf16[4,2048,6144]{2,1,0:T(8,128)(2,1)}), bf16[4,2048,6144]{2,1,0:T(8,128)(2,1)}, u32[]{:S(2)}, u32[]{:S(2)}) async-start(bf16[4,2048,6144]{2,1,0:T(8,128)(2,1)} %bitcast.15), calls=%async_computation.4 | async-start | bytes 201326592 | tf_op jit(solution)/shard_map/all_to_all | solution.py:16
  7331.3 18.9 copy-start.39
  7331.3 19.0 copy-start.40
  7331.3 1100.4 %all-to-all-start.3 = ((bf16[4,2048,6144]{2,1,0:T(8,128)(2,1)}), bf16[4,2048,6144]{2,1,0:T(8,128)(2,1)}, u32[]{:S(2)}, u32[]{:S(2)}) async-start(bf16[4,2048,6144]{2,1,0:T(8,128)(2,1)} %bitcast.14), calls=%async_computation.3 | async-start | bytes 201326592 | tf_op jit(solution)/shard_map/all_to_all | solution.py:16
  7350.2 1749.3 %all-gather.12.cloned.1.call-start = ((), (), s32[]{:S(2)}) async-start(), calls=%async_computation.9 | async-start | bytes 125829120 | tf_op jit(solution)/shard_map/all_gather | solution.py:81
  9214.0 10.2 copy-start.48
  9214.0 192.5 %all-to-all-start.5 = ((bf16[2,4096,1024]{2,1,0:T(8,128)(2,1)}), bf16[2,4096,1024]{2,1,0:T(8,128)(2,1)}, u32[]{:S(2)}, u32[]{:S(2)}) async-start(bf16[2,4096,1024]{2,1,0:T(8,128)(2,1)} %bitcast.50), calls=%async_computation.5 | async-start | bytes 33554432 | tf_op jit(solution)/shard_map/all_to_all | solution.py:16
  9223.9 399.7 %all-gather.14.cloned.1.call-start = ((), (), s32[]{:S(2)}) async-start(), calls=%async_computation.10 | async-start | bytes 25165824 | tf_op jit(solution)/shard_map/all_gather | solution.py:84
  9417.2 220.3 %copy-start.1 = (bf16[11,256,256]{2,1,0:T(8,128)(2,1)S(1)}, bf16[11,256,256]{2,1,0:T(8,128)(2,1)}, u32[]{:S(2)}) copy-start(bf16[11,256,256]{2,1,0:T(8,128)(2,1)} %param.33) | copy-start | bytes 4325380
Sparse Core Ops, SparseCore 0:
  640.7 466.8 all-gather.5
  1452.0 271.2 all-gather.7
  5919.8 195.9 all-gather.9
  8520.6 578.9 all-gather.11
  9428.0 195.5 all-gather.13
where the time goes:
time: 9720 us; the launch traced here: 9640 us
  waiting for transfers between devices  4500 us (46%)
  local copies, waits for them, and re-layouts  3140 us (32%)
  other arithmetic  1280 us (13%)
  matrix products  609 us (6%)
    all_to_all x6, waiting for transfers between devices, token_sum(): received = lax.all_to_all(pieces, axis_name, 0, 0)  3530 us
    slice x74, local copies, waits for them, and re-layouts, rg_lru(): lax.associative_scan(combine, (decay.reshape(seqs, steps, width), drive.r...  1820 us
    pad x22, local copies, waits for them, and re-layouts, rg_lru(): lax.associative_scan(combine, (decay.reshape(seqs, steps, width), drive.r...  676 us
    all_gather x1, waiting for transfers between devices, local_layer(): inner = lax.all_gather(inner_rows, 'wd', axis=0, tiled=True)  579 us
    reshape x3, local copies, waits for them, and re-layouts, rg_lru(): jnp.einsum('nbi,bij->nbj', grouped, rgate_w, preferred_element_type=jnp.f...  338 us
    all_gather x1, waiting for transfers between devices, local_layer(): lax.all_gather(rms_apply(resid, sum_sq2, model_width, gain_mlp), 'ch', ax...  196 us
    all_gather x1, waiting for transfers between devices, local_layer(): return lax.all_gather(out_rows, 'ch', axis=0, tiled=True)  196 us
  transfers between devices with their start and end apart: 11, of which 9 were waited for; matrix products, arithmetic and copies ran while one was open for 46% of the time, Pallas kernels for 0%

commit v1 on v0

v1 whole, which is shorter than its diff:
```python
import jax
import jax.numpy as jnp
from jax import lax
from jax.experimental import pallas as pl
from jax.experimental.pallas import tpu as pltpu
from jax.sharding import PartitionSpec as P


EPS = 1e-6
CHUNKS = 3
ROWS = 128
COLS = 512
TIME_BLOCK = 256


bf16 = jnp.bfloat16
f32 = jnp.float32


def dot(a, b):
    return jnp.dot(a, b, preferred_element_type=f32)


def recurrence_kernel(u_ref, y_ref, pos_ref, conv_w_ref, conv_b_ref, rate_ref, rw_ref, rb_ref, iw_ref, ib_ref, out_ref, ext, dec, drv, carry):
    rows, width = u_ref.shape
    groups = rows // 8

    @pl.when(pl.program_id(1) == 0)
    def _():
        ext[0:8, :] = jnp.zeros((8, width), f32)
        carry[...] = jnp.zeros_like(carry)

    pos = pos_ref[...]
    u = u_ref[...].astype(f32)
    ext[8:8 + rows, :] = u
    taps = conv_w_ref[...].astype(f32)
    total = conv_b_ref[...].astype(f32) + u * taps[0:1]
    for shift in range(1, conv_w_ref.shape[0]):
        total = total + jnp.where(pos >= shift, ext[8 - shift:8 - shift + rows, :], 0.0) * taps[shift:shift + 1]
    ext[0:8, :] = u[rows - 8:rows]
    conv = total.astype(bf16)
    rate = jax.nn.sigmoid(dot(conv, rw_ref[...]) + rb_ref[...].astype(f32))
    inflow = jax.nn.sigmoid(dot(conv, iw_ref[...]) + ib_ref[...].astype(f32))
    log_a = rate * rate_ref[...]
    decay = jnp.exp(log_a)
    scale = jnp.sqrt(-jnp.tanh(log_a) * (decay * decay + 1.0))
    reset = pos == 0
    decay = jnp.where(reset, 0.0, decay)
    scale = jnp.where(reset, 1.0, scale)
    drive = scale * inflow * conv.astype(f32)
    a = decay.reshape(groups, 8, width)
    b = drive.reshape(groups, 8, width)
    row = lax.broadcasted_iota(jnp.int32, (groups, 8, width), 1)
    for step in (1, 2, 4):
        keep = row >= step
        b = a * jnp.where(keep, pltpu.roll(b, step, 1), 0.0) + b
        a = a * jnp.where(keep, pltpu.roll(a, step, 1), 1.0)
    dec[...] = a
    drv[...] = b
    state = carry[0:1, :]
    for group in range(groups):
        hidden = dec[group] * state + drv[group]
        drv[group] = hidden
        state = hidden[7:8, :]
    carry[0:1, :] = state
    out_ref[...] = (drv[...].reshape(rows, width) * y_ref[...].astype(f32)).astype(bf16)


def recurrence(u, y, pos, conv_w, conv_b, rate, rw, rb, iw, ib):
    tokens, width = u.shape
    blocks, block = rw.shape[0], rw.shape[1]
    time_spec = pl.BlockSpec((TIME_BLOCK, block), lambda b, t: (t, b))
    row_spec = pl.BlockSpec((1, block), lambda b, t: (0, b))
    gate_spec = pl.BlockSpec((None, block, block), lambda b, t: (b, 0, 0))
    return pl.pallas_call(
        recurrence_kernel,
        grid=(blocks, tokens // TIME_BLOCK),
        in_specs=[time_spec, time_spec, pl.BlockSpec((TIME_BLOCK, 1), lambda b, t: (t, 0)),
                  pl.BlockSpec((conv_w.shape[0], block), lambda b, t: (0, b)), row_spec, row_spec,
                  gate_spec, row_spec, gate_spec, row_spec],
        out_specs=time_spec,
        out_shape=jax.ShapeDtypeStruct((tokens, width), bf16),
        scratch_shapes=[pltpu.VMEM((TIME_BLOCK + 8, block), f32), pltpu.VMEM((TIME_BLOCK // 8, 8, block), f32),
                        pltpu.VMEM((TIME_BLOCK // 8, 8, block), f32), pltpu.VMEM((8, block), f32)],
        compiler_params=pltpu.CompilerParams(dimension_semantics=("arbitrary", "arbitrary")),
        cost_estimate=pl.CostEstimate(flops=tokens * width * 1200, bytes_accessed=tokens * width * 6, transcendentals=tokens * width * 8),
        name="recurrence",
    )(u, y, pos, conv_w, conv_b[None], rate[None], rw, rb[None], iw, ib[None])


def inner_kernel(m_ref, *refs):
    gate_w, up_w, (gate_b, up_b, out_ref) = refs[:4], refs[4:8], refs[8:]
    depth = gate_w[0].shape[0]
    rows = m_ref.shape[0] // 4

    @pl.loop(0, 4)
    def _(part):
        at = pl.ds(part * rows, rows)

        def product(ws):
            return sum(dot(m_ref[at, j * depth:(j + 1) * depth], w[...]) for j, w in enumerate(ws))

        gate = jax.nn.gelu(product(gate_w) + gate_b[...].astype(f32), approximate=True)
        out_ref[at, :] = (gate * (product(up_w) + up_b[...].astype(f32))).astype(bf16)


def inner_of(m, gate_w, up_w, gate_b, up_b):
    tokens, width = m.shape
    depth, size = gate_w[0].shape
    weight = pl.BlockSpec((depth, COLS), lambda n: (0, n))
    vector = pl.BlockSpec((1, COLS), lambda n: (0, n))
    return pl.pallas_call(
        inner_kernel, grid=(size // COLS,),
        in_specs=[pl.BlockSpec((tokens, width), lambda n: (0, 0))] + [weight] * 8 + [vector] * 2,
        out_specs=pl.BlockSpec((tokens, COLS), lambda n: (0, n)),
        out_shape=jax.ShapeDtypeStruct((tokens, size), bf16),
        cost_estimate=pl.CostEstimate(flops=4 * tokens * width * size, bytes_accessed=4 * width * size + 2 * tokens * (width + size), transcendentals=tokens * size),
        name="inner")(m, *gate_w, *up_w, gate_b[None], up_b[None])


def tie(*values):
    return lax.optimization_barrier(values)


def pick(parts, quarter):
    value = parts[0][...]
    for index in range(1, 4):
        value = jnp.where(quarter == index, parts[index][...], value)
    return value.astype(f32)


def write_norm(pieces, gain_ref, out_ref):
    width = pieces[0].shape[1]
    total = sum(jnp.sum(p * p, axis=1, keepdims=True) for p in pieces)
    inv = lax.rsqrt(total / (width * len(pieces)) + EPS)
    for j, p in enumerate(pieces):
        out_ref[:, j * width:(j + 1) * width] = (p * inv * (1.0 + gain_ref[j:j + 1, :])).astype(bf16)


def norm_kernel(at_ref, own_ref, near_ref, *refs):
    far, diag, (gain_ref, out_ref) = refs[:4], refs[4:8], refs[8:]
    quarter = pl.program_id(0) // (pl.num_programs(0) // 4)
    pieces = [own_ref[...].astype(f32), near_ref[...].astype(f32), pick(far, quarter), pick(diag, quarter)]
    write_norm(pieces, gain_ref, out_ref)


def norm_in(own, near, far, diag, gain):
    tokens, width = own.shape
    rows = 2 * ROWS
    per = tokens // rows // 4
    whole = pl.BlockSpec((rows, width), lambda i, at: (i, 0))
    parts = [pl.BlockSpec((rows, width), lambda i, at, q=q: (jnp.clip(i - q * per, 0, per - 1), 0)) for q in range(4)]
    spec = pltpu.PrefetchScalarGridSpec(
        num_scalar_prefetch=1, grid=(tokens // rows,),
        in_specs=[whole, whole] + parts + parts + [pl.BlockSpec((4, width), lambda i, at: (0, 0))],
        out_specs=pl.BlockSpec((rows, 4 * width), lambda i, at: (i, 0)))
    return pl.pallas_call(
        norm_kernel, grid_spec=spec, out_shape=jax.ShapeDtypeStruct((tokens, 4 * width), bf16),
        cost_estimate=pl.CostEstimate(flops=tokens * width * 600, bytes_accessed=tokens * width * 16, transcendentals=0),
        name="norm_in")(jnp.zeros((1,), jnp.int32), own, near, *far, *diag, gain)


def resid_kernel(at_ref, own_ref, near_ref, *refs):
    far, diag, kept, got = refs[:4], refs[4:8], refs[8:12], refs[12:16]
    bias_ref, gain_ref = refs[16:18]
    out, norm_ref = refs[18:22], refs[22]
    quarter = at_ref[2]
    base = [own_ref[...].astype(f32), near_ref[...].astype(f32), pick(far, quarter), pick(diag, quarter)]
    pieces = [b + (k[...] + g[...].astype(f32)) + bias_ref[j:j + 1, :] for j, (b, k, g) in enumerate(zip(base, kept, got))]
    for o, p in zip(out, pieces):
        o[...] = p
    write_norm(pieces, gain_ref, norm_ref)


def resid_norm(at, own, near, far, diag, kept, got, bias, gain):
    tokens, width = kept[0].shape
    per = tokens // ROWS

    def at_row(k):
        return pl.BlockSpec((ROWS, width), lambda i, at: (at[k] * per + i, 0))

    whole = pl.BlockSpec((ROWS, width), lambda i, at: (i, 0))
    parts = [pl.BlockSpec((ROWS, width), lambda i, at, q=q: (jnp.where(at[2] == q, i, 0), 0)) for q in range(4)]
    vector = pl.BlockSpec((4, width), lambda i, at: (0, 0))
    spec = pltpu.PrefetchScalarGridSpec(
        num_scalar_prefetch=1, grid=(per,),
        in_specs=[at_row(0), at_row(1)] + parts + parts + [whole] * 8 + [vector] * 2,
        out_specs=[whole] * 4 + [pl.BlockSpec((ROWS, 4 * width), lambda i, at: (i, 0))])
    shape = jax.ShapeDtypeStruct((tokens, width), f32)
    out = pl.pallas_call(
        resid_kernel, grid_spec=spec, out_shape=[shape] * 4 + [jax.ShapeDtypeStruct((tokens, 4 * width), bf16)],
        cost_estimate=pl.CostEstimate(flops=tokens * width * 1600, bytes_accessed=tokens * width * 40, transcendentals=0),
        name="resid_norm")(at, own, near, *far, *diag, *kept, *got, bias, gain)
    return out[:4], out[4]


def solution(mesh):
    row_spec = P('dp', 'wd')
    specs = (row_spec, P('dp', None), P('wd'), P('wd', 'ch'), P('ch'), P('wd', 'ch'), P('ch'), P(None, 'ch'), P('ch'), P('ch'), P('ch', None, None), P('ch'), P('ch', None, None), P('ch'), P('ch', 'wd'), P('wd'), P('wd'), P('wd', 'ch'), P('ch'), P('wd', 'ch'), P('ch'), P('ch', 'wd'), P('wd'))

    def pc(a):
        return lax.ppermute(a, 'wd', [(i, i ^ 1) for i in range(4)])

    def over_x(a, flip):
        return lax.ppermute(a, 'wd', [(i, i ^ flip) for i in range(4)])

    def px(a):
        return over_x(a, 2)

    def pd(a):
        return over_x(a, 3)

    def py(a):
        return lax.ppermute(a, 'ch', [(0, 1), (1, 0)])

    def local_layer(resid_in, seg_pos, gain_temporal, w_x, bias_x, w_y, bias_y, conv_w, conv_bias, lam_param, rgate_w, rgate_b, igate_w, igate_b, w_o, bias_o, gain_mlp, w_g, bias_g, w_u, bias_u, w_d, bias_d):
        tokens, local_width = resid_in.shape
        _, steps = seg_pos.shape
        half, quarter = steps // 2, steps // 4
        wd = lax.axis_index('wd')
        cy = lax.axis_index('ch')
        cx, core = wd // 2, wd % 2
        blocks, block = rgate_w.shape[0], rgate_w.shape[1]
        my_blocks = (blocks + 1) // 2
        first_block = core * (blocks - my_blocks)
        other_block = (1 - core) * (blocks - my_blocks)
        lanes = my_blocks * block

        def rows(a, start, size):
            return lax.dynamic_slice_in_dim(a, start, size, axis=0)

        def cols(a, start, size):
            return lax.dynamic_slice_in_dim(a, start, size, axis=a.ndim - 1)

        def my_cols(w):
            return cols(w, first_block * block, lanes)

        x_first = [rows(resid_in, (1 - cx) * steps + cy * half + c * quarter, quarter) for c in range(2)]
        far_mine = [px(a) for a in x_first]
        vec = jnp.stack([gain_temporal, gain_mlp, bias_o, bias_d])
        vecs = [vec, pc(vec), px(vec), pd(vec)]
        x_own = rows(resid_in, cx * steps, steps)
        x_near = pc(x_own)
        shares = []
        for w in (w_y, w_x):
            mine, others = my_cols(w), cols(w, other_block * block, lanes)
            shares.append((mine, pc(others), px(mine), pd(others)))
        wo_far = px(w_o)
        size = w_g.shape[1] // CHUNKS
        parts = [slice(c * size, (c + 1) * size) for c in range(CHUNKS)]
        mlp = []
        for part in parts:
            ws = (w_g[:, part], w_u[:, part], w_d[part])
            mlp.append([(w, pc(w), px(w)) for w in ws])

        table = jnp.stack([v.astype(f32) for v in vecs], axis=1)
        gain_t, gain_m, b_o, b_d = table[0], table[1], table[2], table[3]

        far_other = [py(a) for a in far_mine]
        low = cy == 0

        def quarters(mine, other):
            return [jnp.where(low, m, o) for m, o in zip(mine, other)] + [jnp.where(low, o, m) for m, o in zip(mine, other)]

        far = quarters(far_mine, far_other)
        diag = quarters([pc(a) for a in far_mine], [pc(a) for a in far_other])
        normed = norm_in(x_own, x_near, far, diag, gain_t)

        wy_all = jnp.concatenate(shares[0], axis=0)
        y = jax.nn.gelu(dot(normed, wy_all) + my_cols(bias_y).astype(f32), approximate=True).astype(bf16)
        y, *wx = tie(y, *shares[1])
        u = (dot(normed, jnp.concatenate(wx, axis=0)) + my_cols(bias_x).astype(f32)).astype(bf16)
        rate = -8.0 * jax.nn.softplus(-my_cols(lam_param))
        pos = rows(seg_pos, cx, 1).reshape(steps, 1)
        mixed = recurrence(u, y, pos, my_cols(conv_w), my_cols(conv_bias), rate,
                           rows(rgate_w, first_block, my_blocks), my_cols(rgate_b),
                           rows(igate_w, first_block, my_blocks), my_cols(igate_b))
        mixed, wo_far = tie(mixed, wo_far)

        kept = rows(mixed, core * half, half)
        got = pc(rows(mixed, (1 - core) * half, half))
        first = core == 0
        mixed_all = jnp.concatenate([jnp.where(first, kept, got), jnp.where(first, got, kept)[:, 2 * lanes - blocks * block:]], axis=1)
        wo = [w_o, pc(w_o), wo_far, pc(wo_far)]
        mixed_send = rows(mixed_all, (1 - cy) * quarter, quarter)
        mixed_keep = rows(mixed_all, cy * quarter, quarter)
        received = [py(dot(mixed_send, w).astype(bf16)) for w in wo]
        own = [dot(mixed_keep, w) for w in wo]
        my_quarter = core * 2 + cy
        at = jnp.stack([cx * 4 + my_quarter, my_quarter, my_quarter]).astype(jnp.int32)
        resid, m_own = resid_norm(at, resid_in, x_near, far, diag, own, received, b_o, gain_m)
        m_other = py(m_own)
        m = [m_own, m_other]

        acc = [[None] * 4, [None] * 4]

        def relay(w, far_piece):
            return [w[0], w[1], far_piece, pc(far_piece)]

        def up(s, c, gate_w, up_w):
            return inner_of(m[s], gate_w, up_w, bias_g[parts[c]], bias_u[parts[c]])

        def add_down(s, inner, d_all):
            for j in (3, 2, 1, 0):
                term = dot(inner, d_all[j])
                acc[s][j] = term if acc[s][j] is None else acc[s][j] + term

        def after(s, *extra):
            flat = tie(*acc[s], *extra)
            acc[s] = list(flat[:4])
            return flat[4:]

        (g0, u0, d0), (g1, u1, d1), (g2, u2, d2) = mlp
        m[0], far_g, far_u = tie(m[0], g0[2], u0[2])
        g0, u0 = relay(g0, far_g), relay(u0, far_u)
        inner, far_d = tie(up(0, 0, g0, u0), d0[2])
        d0 = relay(d0, far_d)
        add_down(0, inner, d0)
        far_g, far_u = after(0, g1[2], u1[2])
        g1, u1 = relay(g1, far_g), relay(u1, far_u)
        inner_own, m[1] = tie(up(0, 1, g1, u1), m[1])
        inner, inner_own, far_d = tie(up(1, 0, g0, u0), inner_own, d1[2])
        d1 = relay(d1, far_d)
        add_down(1, inner, d0)
        m[1], = after(1, m[1])
        inner = up(1, 1, g1, u1)
        inner, inner_own = tie(inner, inner_own)
        add_down(0, inner_own, d1)
        add_down(1, inner, d1)
        flat = tie(*acc[0], *acc[1], g2[2], u2[2])
        acc = [list(flat[:4]), list(flat[4:8])]
        g2, u2 = relay(g2, flat[8]), relay(u2, flat[9])
        inner = [up(0, 2, g2, u2), up(1, 2, g2, u2)]
        inner[0], inner[1], far_d = tie(inner[0], inner[1], d2[2])
        d2 = relay(d2, far_d)
        add_down(1, inner[1], d2)
        add_down(0, inner[0], d2)

        down = [None] * 4
        for j in (3, 2, 1, 0):
            down[j] = py(acc[1][j].astype(bf16))
        pieces = []
        for j in (3, 2, 1, 0):
            out = (resid[j] + (acc[0][j] + down[j].astype(f32)) + b_d[j]).astype(bf16)
            moved = out if j == 0 else (pc, lambda a: over_x(a, 2), lambda a: over_x(a, 3))[j - 1](out)
            pieces.append((j, moved, py(moved)))
        result = jnp.zeros((tokens, local_width), bf16)
        for j, mine, other in pieces:
            base = jnp.bitwise_xor(wd, j) * half
            result = lax.dynamic_update_slice_in_dim(result, mine, base + cy * quarter, axis=0)
            result = lax.dynamic_update_slice_in_dim(result, other, base + (1 - cy) * quarter, axis=0)
        return result

    return jax.shard_map(local_layer, mesh=mesh, in_specs=specs, out_specs=row_spec, check_vma=False)
```

time: 9720 us -> 1910 us (0.20)
  waiting for transfers between devices: 4500 us -> 881 us
  local copies, waits for them, and re-layouts: 3140 us -> 95.6 us
  other arithmetic: 1280 us -> 64.9 us
  Pallas kernels: 0 us -> 420 us
  matrix products: 609 us -> 389 us
    all_to_all x6 -> x0, waiting for transfers between devices: 3530 us -> none  [token_sum(): received = lax.all_to_all(pieces, axis_name, 0, 0)]
    slice x78 -> x10, local copies, waits for them, and re-layouts: 1960 us -> 25.2 us  [the longest x3 24 us: local_layer(): ws = (w_g[:, part], w_u[:, part], w_d[part])]
    all_gather x5 -> x0, waiting for transfers between devices: 971 us -> none  [the longest x1 579 us: local_layer(): inner = lax.all_gather(inner_rows, 'wd', axis=0, tiled=True)]
    ppermute x0 -> x65, waiting for transfers between devices: none -> 881 us  [the longest x20 464 us: over_x(): return lax.ppermute(a, 'wd', [(i, i ^ flip) for i in range(4)])]
    pad x22 -> x0, local copies, waits for them, and re-layouts: 676 us -> none  [rg_lru(): lax.associative_scan(combine, (decay.reshape(seqs, steps, width), drive.r...]
    reshape x4 -> x2, local copies, waits for them, and re-layouts: 429 us -> 2.01 us  [local_layer(): pos = rows(seg_pos, cx, 1).reshape(steps, 1)]
    pallas_call x0 -> x9, Pallas kernels: none -> 420 us  [the longest x6 278 us: inner_of(): pl.pallas_call(inner_kernel, grid=(size // COLS,), in_specs=[pl.BlockSpec...]
    add x25 -> x4, other arithmetic: 334 us -> 11.9 us  [add_down(): acc[s][j] = term if acc[s][j] is None else acc[s][j] + term]
  transfers between devices with their start and end apart: 11 -> 65, of which waited for: 9 -> 24; matrix products, arithmetic and copies ran while one was open for 46% -> 28% of each run, Pallas kernels for 0% -> 22%
where the time goes in v1:
time: 1910 us; the launch traced here: 1900 us
  waiting for transfers between devices  881 us (46%)
  Pallas kernels  420 us (22%)
  matrix products  389 us (20%)
  local copies, waits for them, and re-layouts  95.6 us (5%)
  other arithmetic  64.9 us (3%)
  starting transfers between devices  52.5 us (3%)
    ppermute x20, waiting for transfers between devices, over_x(): return lax.ppermute(a, 'wd', [(i, i ^ flip) for i in range(4)])  464 us
    ppermute x15, waiting for transfers between devices, py(): return lax.ppermute(a, 'ch', [(0, 1), (1, 0)])  397 us
    dot_general x34, matrix products, dot(): return jnp.dot(a, b, preferred_element_type=f32)  389 us
    pallas_call x6, Pallas kernels, inner_of(): pl.pallas_call(inner_kernel, grid=(size // COLS,), in_specs=[pl.BlockSpec...  278 us
    pallas_call x1, Pallas kernels, recurrence(): pl.pallas_call(recurrence_kernel, grid=(blocks, tokens // TIME_BLOCK), in...  89.6 us
  transfers between devices with their start and end apart: 65, of which 24 were waited for; matrix products, arithmetic and copies ran while one was open for 28% of the time, Pallas kernels for 22%

profile of v1, /device:TPU:0, one launch (start us, length us, event | category | flops | bytes accessed | tf_op | source)
XLA Modules:
  0.0 1904.4 jit_solution(1434899032112261338)
XLA Ops:
  7.4 7.8 constant_dynamic-slice_fusion.10.own_ref
  15.2 38.9 %collective-permute-done.3 = bf16[1024,1024]{1,0:T(8,128)(2,1)} collective-permute-done((bf16[1024,1024]{1,0:T(8,128)(2,1)}, bf16[1024,1024]{1,0:T(8,128)(2,1)}, u32[]{:S(2)}, u32[]{:S(2)}) %collective-permute-start.3) | collective-permute-done | bytes 2097184 | tf_op jit(solution)/shard_map/ppermute | solution.py:205
  58.8 39.6 %collective-permute-done.10 = bf16[4,1024]{1,0:T(4,128)(2,1)S(1)} collective-permute-done((bf16[4,1024]{1,0:T(4,128)(2,1)S(1)}, bf16[4,1024]{1,0:T(4,128)(2,1)S(1)}, u32[]{:S(2)}, u32[]{:S(2)}) %collective-permute-start.10) | collective-permute-done | bytes 8224 | tf_op jit(solution)/shard_map/ppermute | solution.py:205
  112.3 34.5 %collective-permute-done.2 = bf16[1024,1024]{1,0:T(8,128)(2,1)} collective-permute-done((bf16[1024,1024]{1,0:T(8,128)(2,1)}, bf16[1024,1024]{1,0:T(8,128)(2,1)}, u32[]{:S(2)}, u32[]{:S(2)}) %collective-permute-start.2) | collective-permute-done | bytes 2097184 | tf_op jit(solution)/shard_map/ppermute | solution.py:214
  175.1 30.5 %norm_in.1 = bf16[4096,4096]{1,0:T(8,128)(2,1)} custom-call(s32[1]{0:T(128)} %constant.64.clone.1.at_ref, bf16[4096,1024]{1,0:T(8,128)(2,1)} %constant_dynamic-slice_fusion.10.own_ref, bf16[4096,1024]{1,0:T(8,128)(2,1)} %collective-permute-done.near_ref, bf16[1024,1024]{1,0:T(8,128)(2,1)} %get-tuple-element.127.refs_0_, ...), custom_call_target="tpu_custom_call" | custom-call | flops 2516582400 | bytes 67108864 | tf_op jit(solution)/shard_map/norm_in/pallas_call | solution.py:157
  206.1 79.1 %collective-permute-done.13 = bf16[1024,1536]{1,0:T(8,128)(2,1)} collective-permute-done((bf16[1024,1536]{1,0:T(8,128)(2,1)S(1)}, bf16[1024,1536]{1,0:T(8,128)(2,1)}, u32[]{:S(2)}, u32[]{:S(2)}) %collective-permute-start.13) | collective-permute-done | bytes 3145760 | tf_op jit(solution)/shard_map/ppermute | solution.py:205
  286.3 67.3 %fusion.7.y_ref = bf16[4096,1536]{1,0:T(8,128)(2,1)} fusion(bf16[4096,4096]{1,0:T(8,128)(2,1)} %norm_in.1, bf16[1024,1536]{1,0:T(8,128)(2,1)} %collective-permute-done.14, bf16[1024,1536]{1,0:T(8,128)(2,1)} %collective-permute-done.13, bf16[1024,1536]{1,0:T(8,128)(2,1)} %collective-permute-done.12, bf16[1024,1536]{1,0:T(8,128)(2,1)S(1)} %get-tuple-element.118, ...), kind=kOutput, calls=%fused_computation.8 | convolution fusion | flops 51652853760 | bytes 58726400 | tf_op jit(solution)/shard_map/dot_general | solution.py:21
  353.6 66.5 %collective-permute-done.16 = bf16[1024,1536]{1,0:T(8,128)(2,1)} collective-permute-done((bf16[1024,1536]{1,0:T(8,128)(2,1)}, bf16[1024,1536]{1,0:T(8,128)(2,1)}, u32[]{:S(2)}, u32[]{:S(2)}) %collective-permute-start.16) | collective-permute-done | bytes 3145760 | tf_op jit(solution)/shard_map/ppermute | solution.py:205
  420.0 71.6 %add_convert_fusion.u_ref = bf16[4096,1536]{1,0:T(8,128)(2,1)} fusion(bf16[4096,4096]{1,0:T(8,128)(2,1)} %norm_in.1, bf16[1024,1536]{1,0:T(8,128)(2,1)} %collective-permute-done.17, bf16[1024,1536]{1,0:T(8,128)(2,1)} %collective-permute-done.16, bf16[1024,1536]{1,0:T(8,128)(2,1)} %collective-permute-done.15, bf16[1024,1536]{1,0:T(8,128)(2,1)} %get-tuple-element.53, ...), kind=kOutput, calls=%fused_computation.9 | convolution fusion | flops 51602522112 | bytes 58726400 | tf_op jit(solution)/shard_map/dot_general | solution.py:21
  491.6 89.6 %recurrence.1 = bf16[4096,1536]{1,0:T(8,128)(2,1)} custom-call(bf16[4096,1536]{1,0:T(8,128)(2,1)} %add_convert_fusion.u_ref, bf16[4096,1536]{1,0:T(8,128)(2,1)} %fusion.7.y_ref, s32[4096,1]{1,0:T(8,128)} %copy.28.pos_ref, bf16[4,1536]{1,0:T(4,128)(2,1)} %constant_dynamic-slice_fusion.3.conv_w_ref, bf16[1,1536]{1,0:T(2,128)(2,1)} %broadcast_in_dim.42.conv_b_ref, ...), custom_call_target="tpu_custom_call" | custom-call | flops 7549747200 | bytes 37748736 | tf_op jit(solution)/shard_map/recurrence/pallas_call | solution.py:75
  581.3 6.1 constant_dynamic-slice_fusion
  587.9 9.7 fusion.41
  616.2 8.3 convolution_convert_fusion.1
  624.5 8.1 convolution_convert_fusion
  634.2 8.1 convolution_convert_fusion.3
  642.3 9.5 fusion.46.refs_10_
  651.8 9.5 fusion.44.refs_8_
  661.8 8.1 convolution_convert_fusion.2
  671.4 8.7 collective-permute-done.25.refs_15_
  681.6 9.4 fusion.47.refs_11_
  691.1 9.5 fusion.45.refs_9_
  700.5 24.6 %collective-permute-done.24.refs_14_ = bf16[1024,1024]{1,0:T(8,128)(2,1)} collective-permute-done((bf16[1024,1024]{1,0:T(8,128)(2,1)S(1)}, bf16[1024,1024]{1,0:T(8,128)(2,1)}, u32[]{:S(2)}, u32[]{:S(2)}) %collective-permute-start.24) | collective-permute-done | bytes 2097184 | tf_op jit(solution)/shard_map/ppermute | solution.py:214
  727.4 42.7 %collective-permute-done.23.refs_13_ = bf16[1024,1024]{1,0:T(8,128)(2,1)} collective-permute-done((bf16[1024,1024]{1,0:T(8,128)(2,1)S(1)}, bf16[1024,1024]{1,0:T(8,128)(2,1)}, u32[]{:S(2)}, u32[]{:S(2)}) %collective-permute-start.23) | collective-permute-done | bytes 2097184 | tf_op jit(solution)/shard_map/ppermute | solution.py:214
  772.4 42.7 %collective-permute-done.22.refs_12_ = bf16[1024,1024]{1,0:T(8,128)(2,1)} collective-permute-done((bf16[1024,1024]{1,0:T(8,128)(2,1)S(1)}, bf16[1024,1024]{1,0:T(8,128)(2,1)}, u32[]{:S(2)}, u32[]{:S(2)}) %collective-permute-start.22) | collective-permute-done | bytes 2097184 | tf_op jit(solution)/shard_map/ppermute | solution.py:214
  815.0 21.5 %resid_norm.1 = (f32[1024,1024]{1,0:T(8,128)}, f32[1024,1024]{1,0:T(8,128)}, f32[1024,1024]{1,0:T(8,128)}, f32[1024,1024]{1,0:T(8,128)}, bf16[1024,4096]{1,0:T(8,128)(2,1)}) custom-call(s32[3]{0:T(128)} %pad_add_fusion.at_ref, bf16[8192,1024]{1,0:T(8,128)(2,1)} %own_ref.1, bf16[4096,1024]{1,0:T(8,128)(2,1)} %collective-permute-done.near_ref, ...), custom_call_target="tpu_custom_call" | custom-call | flops 1677721600 | bytes 41943040 | tf_op jit(solution)/shard_map/resid_norm/pallas_call | solution.py:190
  837.5 9.5 fusion.39
  850.6 46.3 %inner.6 = bf16[1024,2048]{1,0:T(8,128)(2,1)} custom-call(bf16[1024,4096]{1,0:T(8,128)(2,1)} %get-tuple-element.62.m_ref, bf16[1024,2048]{1,0:T(8,128)(2,1)} %get-tuple-element.112.refs_0_, bf16[1024,2048]{1,0:T(8,128)(2,1)} %collective-permute-done.28.refs_1_, bf16[1024,2048]{1,0:T(8,128)(2,1)} %collective-permute-done.26.refs_2_, ...), custom_call_target="tpu_custom_call" | custom-call | flops 34359738368 | bytes 46137344 | tf_op jit(solution)/shard_map/inner/pallas_call | solution.py:112
  896.9 43.4 %collective-permute-done.32 = bf16[2048,1024]{1,0:T(8,128)(2,1)} collective-permute-done((bf16[2048,1024]{1,0:T(8,128)(2,1)}, bf16[2048,1024]{1,0:T(8,128)(2,1)}, u32[]{:S(2)}, u32[]{:S(2)}) %collective-permute-start.32) | collective-permute-done | bytes 4194336 | tf_op jit(solution)/shard_map/ppermute | solution.py:205
  942.6 10.2 fusion.49
  952.7 8.3 fusion.37
  961.2 8.2 fusion.48
  977.0 57.0 %collective-permute-done.35.refs_2_ = bf16[1024,2048]{1,0:T(8,128)(2,1)S(1)} collective-permute-done((bf16[1024,2048]{1,0:T(8,128)(2,1)}, bf16[1024,2048]{1,0:T(8,128)(2,1)S(1)}, u32[]{:S(2)}, u32[]{:S(2)}) %collective-permute-start.35) | collective-permute-done | bytes 4194336 | tf_op jit(solution)/shard_map/ppermute | solution.py:205
  1034.0 89.4 %collective-permute-done.36.refs_6_ = bf16[1024,2048]{1,0:T(8,128)(2,1)S(1)} collective-permute-done((bf16[1024,2048]{1,0:T(8,128)(2,1)}, bf16[1024,2048]{1,0:T(8,128)(2,1)S(1)}, u32[]{:S(2)}, u32[]{:S(2)}) %collective-permute-start.36) | collective-permute-done | bytes 4194336 | tf_op jit(solution)/shard_map/ppermute | solution.py:205
  1138.7 46.4 %inner.7 = bf16[1024,2048]{1,0:T(8,128)(2,1)} custom-call(bf16[1024,4096]{1,0:T(8,128)(2,1)} %get-tuple-element.62.m_ref, bf16[1024,2048]{1,0:T(8,128)(2,1)} %get-tuple-element.113.refs_0_, bf16[1024,2048]{1,0:T(8,128)(2,1)} %copy-done.47, bf16[1024,2048]{1,0:T(8,128)(2,1)} %copy-done.44, bf16[1024,2048]{1,0:T(8,128)(2,1)} %copy-done.50, ...), custom_call_target="tpu_custom_call" | custom-call | flops 34359738368 | bytes 46137344 | tf_op jit(solution)/shard_map/inner/pallas_call | solution.py:112
  1186.1 46.3 %inner.8 = bf16[1024,2048]{1,0:T(8,128)(2,1)} custom-call(bf16[1024,4096]{1,0:T(8,128)(2,1)} %collective-permute-done.41.m_ref, bf16[1024,2048]{1,0:T(8,128)(2,1)} %get-tuple-element.112.refs_0_, bf16[1024,2048]{1,0:T(8,128)(2,1)} %collective-permute-done.28.refs_1_, bf16[1024,2048]{1,0:T(8,128)(2,1)} %collective-permute-done.26.refs_2_, ...), custom_call_target="tpu_custom_call" | custom-call | flops 34359738368 | bytes 46137344 | tf_op jit(solution)/shard_map/inner/pallas_call | solution.py:112
  1232.6 10.1 fusion.52
  1242.6 8.3 fusion.35
  1251.0 6.1 fusion.53
  1257.0 8.2 fusion.51
  1265.2 46.3 %inner.9 = bf16[1024,2048]{1,0:T(8,128)(2,1)} custom-call(bf16[1024,4096]{1,0:T(8,128)(2,1)} %collective-permute-done.41.m_ref, bf16[1024,2048]{1,0:T(8,128)(2,1)} %get-tuple-element.113.refs_0_, bf16[1024,2048]{1,0:T(8,128)(2,1)} %copy-done.47, bf16[1024,2048]{1,0:T(8,128)(2,1)} %copy-done.44, bf16[1024,2048]{1,0:T(8,128)(2,1)} %copy-done.50, ...), custom_call_target="tpu_custom_call" | custom-call | flops 34359738368 | bytes 46137344 | tf_op jit(solution)/shard_map/inner/pallas_call | solution.py:112
  1311.5 8.2 fusion.33
  1319.7 6.3 fusion.55
  1326.5 6.5 fusion.54
  1344.0 8.4 convolution_add_fusion.1
  1352.4 8.4 convolution_add_fusion.3
  1360.8 8.7 convolution_add_fusion.2
  1383.0 15.2 collective-permute-done.46.refs_6_
  1411.7 46.3 %inner.11 = bf16[1024,2048]{1,0:T(8,128)(2,1)} custom-call(bf16[1024,4096]{1,0:T(8,128)(2,1)} %collective-permute-done.41.m_ref, bf16[1024,2048]{1,0:T(8,128)(2,1)} %get-tuple-element.111.refs_0_, bf16[1024,2048]{1,0:T(8,128)(2,1)} %collective-permute-done.47.refs_1_, bf16[1024,2048]{1,0:T(8,128)(2,1)} %collective-permute-done.45.refs_2_, ...), custom_call_target="tpu_custom_call" | custom-call | flops 34359738368 | bytes 46137344 | tf_op jit(solution)/shard_map/inner/pallas_call | solution.py:112
  1458.0 46.3 %inner.10 = bf16[1024,2048]{1,0:T(8,128)(2,1)} custom-call(bf16[1024,4096]{1,0:T(8,128)(2,1)} %get-tuple-element.62.m_ref, bf16[1024,2048]{1,0:T(8,128)(2,1)} %get-tuple-element.111.refs_0_, bf16[1024,2048]{1,0:T(8,128)(2,1)} %collective-permute-done.47.refs_1_, bf16[1024,2048]{1,0:T(8,128)(2,1)} %collective-permute-done.45.refs_2_, ...), custom_call_target="tpu_custom_call" | custom-call | flops 34359738368 | bytes 46137344 | tf_op jit(solution)/shard_map/inner/pallas_call | solution.py:112
  1504.5 7.8 fusion.62
  1515.1 6.3 fusion.60
  1531.2 8.1 fusion.59
  1539.3 67.7 %collective-permute-done.56 = bf16[1024,1024]{1,0:T(8,128)(2,1)S(1)} collective-permute-done((bf16[1024,1024]{1,0:T(8,128)(2,1)S(1)}, bf16[1024,1024]{1,0:T(8,128)(2,1)S(1)}, u32[]{:S(2)}, u32[]{:S(2)}) %collective-permute-start.56) | collective-permute-done | bytes 2097184 | tf_op jit(solution)/shard_map/ppermute | solution.py:214
  1613.0 8.0 fusion.57
  1620.9 30.5 %collective-permute-done.53 = bf16[1024,1024]{1,0:T(8,128)(2,1)} collective-permute-done((bf16[1024,1024]{1,0:T(8,128)(2,1)}, bf16[1024,1024]{1,0:T(8,128)(2,1)}, u32[]{:S(2)}, u32[]{:S(2)}) %collective-permute-start.53) | collective-permute-done | bytes 2097184 | tf_op jit(solution)/shard_map/ppermute | solution.py:214
  1656.4 7.6 fusion.61
  1669.1 35.2 %collective-permute-done.54 = bf16[1024,1024]{1,0:T(8,128)(2,1)} collective-permute-done((bf16[1024,1024]{1,0:T(8,128)(2,1)}, bf16[1024,1024]{1,0:T(8,128)(2,1)}, u32[]{:S(2)}, u32[]{:S(2)}) %collective-permute-start.54) | collective-permute-done | bytes 2097184 | tf_op jit(solution)/shard_map/ppermute | solution.py:205
  1705.8 7.5 fusion.28
  1717.5 7.7 fusion.30
  1725.2 6.1 broadcast_in_dim.41
  1734.4 26.9 %collective-permute-done.55 = bf16[1024,1024]{1,0:T(8,128)(2,1)} collective-permute-done((bf16[1024,1024]{1,0:T(8,128)(2,1)}, bf16[1024,1024]{1,0:T(8,128)(2,1)}, u32[]{:S(2)}, u32[]{:S(2)}) %collective-permute-start.55) | collective-permute-done | bytes 2097184 | tf_op jit(solution)/shard_map/ppermute | solution.py:214
  1773.8 32.5 %collective-permute-done.62 = bf16[1024,1024]{1,0:T(8,128)(2,1)} collective-permute-done((bf16[1024,1024]{1,0:T(8,128)(2,1)}, bf16[1024,1024]{1,0:T(8,128)(2,1)}, u32[]{:S(2)}, u32[]{:S(2)}) %collective-permute-start.62) | collective-permute-done | bytes 2097184 | tf_op jit(solution)/shard_map/ppermute | solution.py:214
  1809.3 40.9 %collective-permute-done.63 = bf16[1024,1024]{1,0:T(8,128)(2,1)} collective-permute-done((bf16[1024,1024]{1,0:T(8,128)(2,1)}, bf16[1024,1024]{1,0:T(8,128)(2,1)}, u32[]{:S(2)}, u32[]{:S(2)}) %collective-permute-start.63) | collective-permute-done | bytes 2097184 | tf_op jit(solution)/shard_map/ppermute | solution.py:214
  1857.2 45.4 %collective-permute-done.64 = bf16[1024,1024]{1,0:T(8,128)(2,1)S(1)} collective-permute-done((bf16[1024,1024]{1,0:T(8,128)(2,1)}, bf16[1024,1024]{1,0:T(8,128)(2,1)S(1)}, u32[]{:S(2)}, u32[]{:S(2)}) %collective-permute-start.64) | collective-permute-done | bytes 2097184 | tf_op jit(solution)/shard_map/ppermute | solution.py:214
  (323 shorter events, 214.8 us)
Async XLA Ops:
  4.1 50.1 %collective-permute-start.3 = (bf16[1024,1024]{1,0:T(8,128)(2,1)}, bf16[1024,1024]{1,0:T(8,128)(2,1)}, u32[]{:S(2)}, u32[]{:S(2)}) collective-permute-start(bf16[1024,1024]{1,0:T(8,128)(2,1)} %get-tuple-element.103), channel_id=1, source_target_pairs={{0,2},{1,3},{2,0},{3,1},{4,6},{5,7},{6,4},{7,5}} | collective-permute-start | bytes 6291464 | tf_op jit(solution)/shard_map/ppermute | solution.py:205
  15.2 158.7 %collective-permute-start = (bf16[4096,1024]{1,0:T(8,128)(2,1)}, bf16[4096,1024]{1,0:T(8,128)(2,1)}, u32[]{:S(2)}, u32[]{:S(2)}) collective-permute-start(bf16[4096,1024]{1,0:T(8,128)(2,1)} %constant_dynamic-slice_fusion.10.own_ref), channel_id=1, source_target_pairs={{0,1},{1,0},{2,3},{3,2},{4,5},{5,4},{6,7},{7,6}} | collective-permute-start | bytes 25165832 | tf_op jit(solution)/shard_map/ppermute | solution.py:202
  15.2 83.2 %collective-permute-start.1 = (bf16[1024,1024]{1,0:T(8,128)(2,1)S(1)}, bf16[1024,1024]{1,0:T(8,128)(2,1)}, u32[]{:S(2)}, u32[]{:S(2)}) collective-permute-start(bf16[1024,1024]{1,0:T(8,128)(2,1)S(1)} %get-tuple-element.104), channel_id=1, source_target_pairs={{0,2},{1,3},{2,0},{3,1},{4,6},{5,7},{6,4},{7,5}} | collective-permute-start | bytes 6291464 | tf_op jit(solution)/shard_map/ppermute | solution.py:205
  54.2 46.3 %collective-permute-start.4 = (bf16[1024,1024]{1,0:T(8,128)(2,1)}, bf16[1024,1024]{1,0:T(8,128)(2,1)}, u32[]{:S(2)}, u32[]{:S(2)}) collective-permute-start(bf16[1024,1024]{1,0:T(8,128)(2,1)} %collective-permute-done.3), channel_id=1, source_target_pairs={{0,4},{4,0},{1,5},{5,1},{2,6},{6,2},{3,7},{7,3}} | collective-permute-start | bytes 6291464 | tf_op jit(solution)/shard_map/ppermute | solution.py:214
  56.4 42.1 %collective-permute-start.10 = (bf16[4,1024]{1,0:T(4,128)(2,1)S(1)}, bf16[4,1024]{1,0:T(4,128)(2,1)S(1)}, u32[]{:S(2)}, u32[]{:S(2)}) collective-permute-start(bf16[4,1024]{1,0:T(4,128)(2,1)S(1)} %pad_maximum_fusion.3), channel_id=1, source_target_pairs={{0,2},{1,3},{2,0},{3,1},{4,6},{5,7},{6,4},{7,5}} | collective-permute-start | bytes 24584 | tf_op jit(solution)/shard_map/ppermute | solution.py:205
  57.9 42.4 %collective-permute-start.11 = (bf16[4,1024]{1,0:T(4,128)(2,1)S(1)}, bf16[4,1024]{1,0:T(4,128)(2,1)S(1)}, u32[]{:S(2)}, u32[]{:S(2)}) collective-permute-start(bf16[4,1024]{1,0:T(4,128)(2,1)S(1)} %pad_maximum_fusion.3), channel_id=1, source_target_pairs={{0,3},{1,2},{2,1},{3,0},{4,7},{5,6},{6,5},{7,4}} | collective-permute-start | bytes 24584 | tf_op jit(solution)/shard_map/ppermute | solution.py:205
  98.4 13.7 collective-permute-start.7
  98.4 48.4 %collective-permute-start.2 = (bf16[1024,1024]{1,0:T(8,128)(2,1)}, bf16[1024,1024]{1,0:T(8,128)(2,1)}, u32[]{:S(2)}, u32[]{:S(2)}) collective-permute-start(bf16[1024,1024]{1,0:T(8,128)(2,1)} %collective-permute-done.1), channel_id=1, source_target_pairs={{0,4},{4,0},{1,5},{5,1},{2,6},{6,2},{3,7},{7,3}} | collective-permute-start | bytes 6291464 | tf_op jit(solution)/shard_map/ppermute | solution.py:214
  100.2 47.5 %collective-permute-start.5 = (bf16[1024,1024]{1,0:T(8,128)(2,1)}, bf16[1024,1024]{1,0:T(8,128)(2,1)}, u32[]{:S(2)}, u32[]{:S(2)}) collective-permute-start(bf16[1024,1024]{1,0:T(8,128)(2,1)} %collective-permute-done.1), channel_id=1, source_target_pairs={{0,1},{1,0},{2,3},{3,2},{4,5},{5,4},{6,7},{7,6}} | collective-permute-start | bytes 6291464 | tf_op jit(solution)/shard_map/ppermute | solution.py:202
  100.4 51.6 %collective-permute-start.8 = (bf16[1024,1024]{1,0:T(8,128)(2,1)}, bf16[1024,1024]{1,0:T(8,128)(2,1)}, u32[]{:S(2)}, u32[]{:S(2)}) collective-permute-start(bf16[1024,1024]{1,0:T(8,128)(2,1)} %collective-permute-done.4), channel_id=1, source_target_pairs={{0,1},{1,0},{2,3},{3,2},{4,5},{5,4},{6,7},{7,6}} | collective-permute-start | bytes 6291464 | tf_op jit(solution)/shard_map/ppermute | solution.py:202
  112.1 93.5 %collective-permute-start.12 = (bf16[1024,1536]{1,0:T(8,128)(2,1)}, bf16[1024,1536]{1,0:T(8,128)(2,1)}, u32[]{:S(2)}, u32[]{:S(2)}) collective-permute-start(bf16[1024,1536]{1,0:T(8,128)(2,1)} %get-tuple-element.119), channel_id=1, source_target_pairs={{0,1},{1,0},{2,3},{3,2},{4,5},{5,4},{6,7},{7,6}} | collective-permute-start | bytes 9437192 | tf_op jit(solution)/shard_map/ppermute | solution.py:202
  146.8 139.5 %collective-permute-start.14 = (bf16[1024,1536]{1,0:T(8,128)(2,1)}, bf16[1024,1536]{1,0:T(8,128)(2,1)}, u32[]{:S(2)}, u32[]{:S(2)}) collective-permute-start(bf16[1024,1536]{1,0:T(8,128)(2,1)} %get-tuple-element.119), channel_id=1, source_target_pairs={{0,3},{1,2},{2,1},{3,0},{4,7},{5,6},{6,5},{7,4}} | collective-permute-start | bytes 9437192 | tf_op jit(solution)/shard_map/ppermute | solution.py:205
  147.8 137.4 %collective-permute-start.13 = (bf16[1024,1536]{1,0:T(8,128)(2,1)S(1)}, bf16[1024,1536]{1,0:T(8,128)(2,1)}, u32[]{:S(2)}, u32[]{:S(2)}) collective-permute-start(bf16[1024,1536]{1,0:T(8,128)(2,1)S(1)} %get-tuple-element.118), channel_id=1, source_target_pairs={{0,2},{1,3},{2,0},{3,1},{4,6},{5,7},{6,4},{7,5}} | collective-permute-start | bytes 9437192 | tf_op jit(solution)/shard_map/ppermute | solution.py:205
  152.1 16.9 collective-permute-start.6
  169.0 184.6 %collective-permute-start.15 = (bf16[1024,1536]{1,0:T(8,128)(2,1)}, bf16[1024,1536]{1,0:T(8,128)(2,1)}, u32[]{:S(2)}, u32[]{:S(2)}) collective-permute-start(bf16[1024,1536]{1,0:T(8,128)(2,1)} %get-tuple-element.116), channel_id=1, source_target_pairs={{0,1},{1,0},{2,3},{3,2},{4,5},{5,4},{6,7},{7,6}} | collective-permute-start | bytes 9437192 | tf_op jit(solution)/shard_map/ppermute | solution.py:202
  173.9 246.1 %collective-permute-start.17 = (bf16[1024,1536]{1,0:T(8,128)(2,1)}, bf16[1024,1536]{1,0:T(8,128)(2,1)}, u32[]{:S(2)}, u32[]{:S(2)}) collective-permute-start(bf16[1024,1536]{1,0:T(8,128)(2,1)} %get-tuple-element.116), channel_id=1, source_target_pairs={{0,3},{1,2},{2,1},{3,0},{4,7},{5,6},{6,5},{7,4}} | collective-permute-start | bytes 9437192 | tf_op jit(solution)/shard_map/ppermute | solution.py:205
  205.6 214.5 %collective-permute-start.16 = (bf16[1024,1536]{1,0:T(8,128)(2,1)}, bf16[1024,1536]{1,0:T(8,128)(2,1)}, u32[]{:S(2)}, u32[]{:S(2)}) collective-permute-start(bf16[1024,1536]{1,0:T(8,128)(2,1)} %get-tuple-element.53), channel_id=1, source_target_pairs={{0,2},{1,3},{2,0},{3,1},{4,6},{5,7},{6,4},{7,5}} | collective-permute-start | bytes 9437192 | tf_op jit(solution)/shard_map/ppermute | solution.py:205
  285.2 296.1 %collective-permute-start.18 = (bf16[2816,1024]{1,0:T(8,128)(2,1)}, bf16[2816,1024]{1,0:T(8,128)(2,1)}, u32[]{:S(2)}, u32[]{:S(2)}) collective-permute-start(bf16[2816,1024]{1,0:T(8,128)(2,1)} %param.37), channel_id=1, source_target_pairs={{0,2},{1,3},{2,0},{3,1},{4,6},{5,7},{6,4},{7,5}} | collective-permute-start | bytes 17301512 | tf_op jit(solution)/shard_map/ppermute | solution.py:205
  587.4 18.1 collective-permute-start.19
  587.4 74.4 %collective-permute-start.20 = (bf16[2816,1024]{1,0:T(8,128)(2,1)}, bf16[2816,1024]{1,0:T(8,128)(2,1)}, u32[]{:S(2)}, u32[]{:S(2)}) collective-permute-start(bf16[2816,1024]{1,0:T(8,128)(2,1)} %param.37), channel_id=1, source_target_pairs={{0,1},{1,0},{2,3},{3,2},{4,5},{5,4},{6,7},{7,6}} | collective-permute-start | bytes 17301512 | tf_op jit(solution)/shard_map/ppermute | solution.py:202
  597.6 238.9 %collective-permute-start.26 = (bf16[1024,2048]{1,0:T(8,128)(2,1)}, bf16[1024,2048]{1,0:T(8,128)(2,1)}, u32[]{:S(2)}, u32[]{:S(2)}) collective-permute-start(bf16[1024,2048]{1,0:T(8,128)(2,1)} %get-tuple-element.112.refs_0_), channel_id=1, source_target_pairs={{0,2},{1,3},{2,0},{3,1},{4,6},{5,7},{6,4},{7,5}} | collective-permute-start | bytes 12582920 | tf_op jit(solution)/shard_map/ppermute | solution.py:205
  598.7 25.8 %collective-permute-start.21 = (bf16[2816,1024]{1,0:T(8,128)(2,1)}, bf16[2816,1024]{1,0:T(8,128)(2,1)}, u32[]{:S(2)}, u32[]{:S(2)}) collective-permute-start(bf16[2816,1024]{1,0:T(8,128)(2,1)} %collective-permute-done.18), channel_id=1, source_target_pairs={{0,1},{1,0},{2,3},{3,2},{4,5},{5,4},{6,7},{7,6}} | collective-permute-start | bytes 17301512 | tf_op jit(solution)/shard_map/ppermute | solution.py:202
  603.7 232.8 %collective-permute-start.27 = (bf16[1024,2048]{1,0:T(8,128)(2,1)}, bf16[1024,2048]{1,0:T(8,128)(2,1)}, u32[]{:S(2)}, u32[]{:S(2)}) collective-permute-start(bf16[1024,2048]{1,0:T(8,128)(2,1)} %get-tuple-element.109.refs_4_), channel_id=1, source_target_pairs={{0,2},{1,3},{2,0},{3,1},{4,6},{5,7},{6,4},{7,5}} | collective-permute-start | bytes 12582920 | tf_op jit(solution)/shard_map/ppermute | solution.py:205
  632.7 47.5 %collective-permute-start.25 = (bf16[1024,1024]{1,0:T(8,128)(2,1)S(1)}, bf16[1024,1024]{1,0:T(8,128)(2,1)S(1)}, u32[]{:S(2)}, u32[]{:S(2)}) collective-permute-start(bf16[1024,1024]{1,0:T(8,128)(2,1)S(1)} %convolution_convert_fusion), channel_id=1, source_target_pairs={{0,4},{4,0},{1,5},{5,1},{2,6},{6,2},{3,7},{7,3}} | collective-permute-start | bytes 6291464 | tf_op jit(solution)/shard_map/ppermute | solution.py:214
  661.3 63.9 %collective-permute-start.24 = (bf16[1024,1024]{1,0:T(8,128)(2,1)S(1)}, bf16[1024,1024]{1,0:T(8,128)(2,1)}, u32[]{:S(2)}, u32[]{:S(2)}) collective-permute-start(bf16[1024,1024]{1,0:T(8,128)(2,1)S(1)} %convolution_convert_fusion.1), channel_id=1, source_target_pairs={{0,4},{4,0},{1,5},{5,1},{2,6},{6,2},{3,7},{7,3}} | collective-permute-start | bytes 6291464 | tf_op jit(solution)/shard_map/ppermute | solution.py:214
  669.9 100.2 %collective-permute-start.23 = (bf16[1024,1024]{1,0:T(8,128)(2,1)S(1)}, bf16[1024,1024]{1,0:T(8,128)(2,1)}, u32[]{:S(2)}, u32[]{:S(2)}) collective-permute-start(bf16[1024,1024]{1,0:T(8,128)(2,1)S(1)} %convolution_convert_fusion.2), channel_id=1, source_target_pairs={{0,4},{4,0},{1,5},{5,1},{2,6},{6,2},{3,7},{7,3}} | collective-permute-start | bytes 6291464 | tf_op jit(solution)/shard_map/ppermute | solution.py:214
  680.1 134.9 %collective-permute-start.22 = (bf16[1024,1024]{1,0:T(8,128)(2,1)S(1)}, bf16[1024,1024]{1,0:T(8,128)(2,1)}, u32[]{:S(2)}, u32[]{:S(2)}) collective-permute-start(bf16[1024,1024]{1,0:T(8,128)(2,1)S(1)} %convolution_convert_fusion.3), channel_id=1, source_target_pairs={{0,4},{4,0},{1,5},{5,1},{2,6},{6,2},{3,7},{7,3}} | collective-permute-start | bytes 6291464 | tf_op jit(solution)/shard_map/ppermute | solution.py:214
  725.2 125.2 %collective-permute-start.28 = (bf16[1024,2048]{1,0:T(8,128)(2,1)}, bf16[1024,2048]{1,0:T(8,128)(2,1)}, u32[]{:S(2)}, u32[]{:S(2)}) collective-permute-start(bf16[1024,2048]{1,0:T(8,128)(2,1)} %get-tuple-element.112.refs_0_), channel_id=1, source_target_pairs={{0,1},{1,0},{2,3},{3,2},{4,5},{5,4},{6,7},{7,6}} | collective-permute-start | bytes 12582920 | tf_op jit(solution)/shard_map/ppermute | solution.py:202
  770.1 80.5 %collective-permute-start.30 = (bf16[1024,2048]{1,0:T(8,128)(2,1)}, bf16[1024,2048]{1,0:T(8,128)(2,1)}, u32[]{:S(2)}, u32[]{:S(2)}) collective-permute-start(bf16[1024,2048]{1,0:T(8,128)(2,1)} %get-tuple-element.109.refs_4_), channel_id=1, source_target_pairs={{0,1},{1,0},{2,3},{3,2},{4,5},{5,4},{6,7},{7,6}} | collective-permute-start | bytes 12582920 | tf_op jit(solution)/shard_map/ppermute | solution.py:202
  836.6 14.0 collective-permute-start.29
  837.5 13.1 collective-permute-start.31
  847.0 93.3 %collective-permute-start.32 = (bf16[2048,1024]{1,0:T(8,128)(2,1)}, bf16[2048,1024]{1,0:T(8,128)(2,1)}, u32[]{:S(2)}, u32[]{:S(2)}) collective-permute-start(bf16[2048,1024]{1,0:T(8,128)(2,1)} %get-tuple-element.106), channel_id=1, source_target_pairs={{0,2},{1,3},{2,0},{3,1},{4,6},{5,7},{6,4},{7,5}} | collective-permute-start | bytes 12582920 | tf_op jit(solution)/shard_map/ppermute | solution.py:205
  850.4 110.6 %collective-permute-start.33 = (bf16[2048,1024]{1,0:T(8,128)(2,1)}, bf16[2048,1024]{1,0:T(8,128)(2,1)}, u32[]{:S(2)}, u32[]{:S(2)}) collective-permute-start(bf16[2048,1024]{1,0:T(8,128)(2,1)} %get-tuple-element.106), channel_id=1, source_target_pairs={{0,1},{1,0},{2,3},{3,2},{4,5},{5,4},{6,7},{7,6}} | collective-permute-start | bytes 12582920 | tf_op jit(solution)/shard_map/ppermute | solution.py:202
  940.3 29.1 %collective-permute-start.34 = (bf16[2048,1024]{1,0:T(8,128)(2,1)}, bf16[2048,1024]{1,0:T(8,128)(2,1)S(1)}, u32[]{:S(2)}, u32[]{:S(2)}) collective-permute-start(bf16[2048,1024]{1,0:T(8,128)(2,1)} %collective-permute-done.32), channel_id=1, source_target_pairs={{0,1},{1,0},{2,3},{3,2},{4,5},{5,4},{6,7},{7,6}} | collective-permute-start | bytes 12582920 | tf_op jit(solution)/shard_map/ppermute | solution.py:202
  940.3 93.7 %collective-permute-start.35 = (bf16[1024,2048]{1,0:T(8,128)(2,1)}, bf16[1024,2048]{1,0:T(8,128)(2,1)S(1)}, u32[]{:S(2)}, u32[]{:S(2)}) collective-permute-start(bf16[1024,2048]{1,0:T(8,128)(2,1)} %get-tuple-element.113.refs_0_), channel_id=1, source_target_pairs={{0,2},{1,3},{2,0},{3,1},{4,6},{5,7},{6,4},{7,5}} | collective-permute-start | bytes 12582920 | tf_op jit(solution)/shard_map/ppermute | solution.py:205
  941.3 184.2 %collective-permute-start.37 = (bf16[1024,2048]{1,0:T(8,128)(2,1)}, bf16[1024,2048]{1,0:T(8,128)(2,1)S(1)}, u32[]{:S(2)}, u32[]{:S(2)}) collective-permute-start(bf16[1024,2048]{1,0:T(8,128)(2,1)} %get-tuple-element.113.refs_0_), channel_id=1, source_target_pairs={{0,1},{1,0},{2,3},{3,2},{4,5},{5,4},{6,7},{7,6}} | collective-permute-start | bytes 12582920 | tf_op jit(solution)/shard_map/ppermute | solution.py:202
  941.5 181.9 %collective-permute-start.36 = (bf16[1024,2048]{1,0:T(8,128)(2,1)}, bf16[1024,2048]{1,0:T(8,128)(2,1)S(1)}, u32[]{:S(2)}, u32[]{:S(2)}) collective-permute-start(bf16[1024,2048]{1,0:T(8,128)(2,1)} %get-tuple-element.110.refs_4_), channel_id=1, source_target_pairs={{0,2},{1,3},{2,0},{3,1},{4,6},{5,7},{6,4},{7,5}} | collective-permute-start | bytes 12582920 | tf_op jit(solution)/shard_map/ppermute | solution.py:205
  961.0 165.4 %collective-permute-start.39 = (bf16[1024,2048]{1,0:T(8,128)(2,1)S(1)}, bf16[1024,2048]{1,0:T(8,128)(2,1)S(1)}, u32[]{:S(2)}, u32[]{:S(2)}) collective-permute-start(bf16[1024,2048]{1,0:T(8,128)(2,1)S(1)} %copy-done.18), channel_id=1, source_target_pairs={{0,1},{1,0},{2,3},{3,2},{4,5},{5,4},{6,7},{7,6}} | collective-permute-start | bytes 12582920 | tf_op jit(solution)/shard_map/ppermute | solution.py:202
  969.4 215.7 %collective-permute-start.41 = (bf16[1024,4096]{1,0:T(8,128)(2,1)}, bf16[1024,4096]{1,0:T(8,128)(2,1)}, u32[]{:S(2)}, u32[]{:S(2)}) collective-permute-start(bf16[1024,4096]{1,0:T(8,128)(2,1)} %get-tuple-element.62.m_ref), channel_id=1, source_target_pairs={{0,4},{4,0},{1,5},{5,1},{2,6},{6,2},{3,7},{7,3}} | collective-permute-start | bytes 25165832 | tf_op jit(solution)/shard_map/ppermute | solution.py:214
  1123.4 7.2 collective-permute-start.38
  1123.4 13.2 collective-permute-start.40
  1125.5 106.9 %collective-permute-start.42 = (bf16[2048,1024]{1,0:T(8,128)(2,1)}, bf16[2048,1024]{1,0:T(8,128)(2,1)}, u32[]{:S(2)}, u32[]{:S(2)}) collective-permute-start(bf16[2048,1024]{1,0:T(8,128)(2,1)} %get-tuple-element.107), channel_id=1, source_target_pairs={{0,2},{1,3},{2,0},{3,1},{4,6},{5,7},{6,4},{7,5}} | collective-permute-start | bytes 12582920 | tf_op jit(solution)/shard_map/ppermute | solution.py:205
  1126.5 199.5 %collective-permute-start.43 = (bf16[2048,1024]{1,0:T(8,128)(2,1)}, bf16[2048,1024]{1,0:T(8,128)(2,1)}, u32[]{:S(2)}, u32[]{:S(2)}) collective-permute-start(bf16[2048,1024]{1,0:T(8,128)(2,1)} %get-tuple-element.107), channel_id=1, source_target_pairs={{0,1},{1,0},{2,3},{3,2},{4,5},{5,4},{6,7},{7,6}} | collective-permute-start | bytes 12582920 | tf_op jit(solution)/shard_map/ppermute | solution.py:202
  1130.6 252.4 %collective-permute-start.45 = (bf16[1024,2048]{1,0:T(8,128)(2,1)}, bf16[1024,2048]{1,0:T(8,128)(2,1)}, u32[]{:S(2)}, u32[]{:S(2)}) collective-permute-start(bf16[1024,2048]{1,0:T(8,128)(2,1)} %get-tuple-element.111.refs_0_), channel_id=1, source_target_pairs={{0,2},{1,3},{2,0},{3,1},{4,6},{5,7},{6,4},{7,5}} | collective-permute-start | bytes 12582920 | tf_op jit(solution)/shard_map/ppermute | solution.py:205
  1138.5 262.3 %collective-permute-start.47 = (bf16[1024,2048]{1,0:T(8,128)(2,1)}, bf16[1024,2048]{1,0:T(8,128)(2,1)}, u32[]{:S(2)}, u32[]{:S(2)}) collective-permute-start(bf16[1024,2048]{1,0:T(8,128)(2,1)} %get-tuple-element.111.refs_0_), channel_id=1, source_target_pairs={{0,1},{1,0},{2,3},{3,2},{4,5},{5,4},{6,7},{7,6}} | collective-permute-start | bytes 12582920 | tf_op jit(solution)/shard_map/ppermute | solution.py:202
  1185.1 213.0 %collective-permute-start.46 = (bf16[1024,2048]{1,0:T(8,128)(2,1)}, bf16[1024,2048]{1,0:T(8,128)(2,1)}, u32[]{:S(2)}, u32[]{:S(2)}) collective-permute-start(bf16[1024,2048]{1,0:T(8,128)(2,1)} %get-tuple-element.108.refs_4_), channel_id=1, source_target_pairs={{0,2},{1,3},{2,0},{3,1},{4,6},{5,7},{6,4},{7,5}} | collective-permute-start | bytes 12582920 | tf_op jit(solution)/shard_map/ppermute | solution.py:205
  1232.4 168.4 %collective-permute-start.49 = (bf16[1024,2048]{1,0:T(8,128)(2,1)}, bf16[1024,2048]{1,0:T(8,128)(2,1)}, u32[]{:S(2)}, u32[]{:S(2)}) collective-permute-start(bf16[1024,2048]{1,0:T(8,128)(2,1)} %get-tuple-element.108.refs_4_), channel_id=1, source_target_pairs={{0,1},{1,0},{2,3},{3,2},{4,5},{5,4},{6,7},{7,6}} | collective-permute-start | bytes 12582920 | tf_op jit(solution)/shard_map/ppermute | solution.py:202
  1326.0 43.5 %collective-permute-start.44 = (bf16[2048,1024]{1,0:T(8,128)(2,1)}, bf16[2048,1024]{1,0:T(8,128)(2,1)S(1)}, u32[]{:S(2)}, u32[]{:S(2)}) collective-permute-start(bf16[2048,1024]{1,0:T(8,128)(2,1)} %collective-permute-done.42), channel_id=1, source_target_pairs={{0,1},{1,0},{2,3},{3,2},{4,5},{5,4},{6,7},{7,6}} | collective-permute-start | bytes 12582920 | tf_op jit(solution)/shard_map/ppermute | solution.py:202
  1398.2 7.5 collective-permute-start.48
  1398.2 13.5 collective-permute-start.50
  1398.7 105.6 %collective-permute-start.51 = (bf16[2048,1024]{1,0:T(8,128)(2,1)}, bf16[2048,1024]{1,0:T(8,128)(2,1)}, u32[]{:S(2)}, u32[]{:S(2)}) collective-permute-start(bf16[2048,1024]{1,0:T(8,128)(2,1)} %get-tuple-element.105), channel_id=1, source_target_pairs={{0,2},{1,3},{2,0},{3,1},{4,6},{5,7},{6,4},{7,5}} | collective-permute-start | bytes 12582920 | tf_op jit(solution)/shard_map/ppermute | solution.py:205
  1400.8 103.7 %collective-permute-start.59 = (bf16[2048,1024]{1,0:T(8,128)(2,1)}, bf16[2048,1024]{1,0:T(8,128)(2,1)}, u32[]{:S(2)}, u32[]{:S(2)}) collective-permute-start(bf16[2048,1024]{1,0:T(8,128)(2,1)} %get-tuple-element.105), channel_id=1, source_target_pairs={{0,1},{1,0},{2,3},{3,2},{4,5},{5,4},{6,7},{7,6}} | collective-permute-start | bytes 12582920 | tf_op jit(solution)/shard_map/ppermute | solution.py:202
  1504.3 19.5 %collective-permute-start.52 = (bf16[2048,1024]{1,0:T(8,128)(2,1)}, bf16[2048,1024]{1,0:T(8,128)(2,1)S(1)}, u32[]{:S(2)}, u32[]{:S(2)}) collective-permute-start(bf16[2048,1024]{1,0:T(8,128)(2,1)} %collective-permute-done.51), channel_id=1, source_target_pairs={{0,1},{1,0},{2,3},{3,2},{4,5},{5,4},{6,7},{7,6}} | collective-permute-start | bytes 12582920 | tf_op jit(solution)/shard_map/ppermute | solution.py:202
  1513.5 150.5 %collective-permute-start.60 = (bf16[1024,1024]{1,0:T(8,128)(2,1)S(1)}, bf16[1024,1024]{1,0:T(8,128)(2,1)S(1)}, u32[]{:S(2)}, u32[]{:S(2)}) collective-permute-start(bf16[1024,1024]{1,0:T(8,128)(2,1)S(1)} %add_convert_fusion.4), channel_id=1, source_target_pairs={{0,4},{4,0},{1,5},{5,1},{2,6},{6,2},{3,7},{7,3}} | collective-permute-start | bytes 6291464 | tf_op jit(solution)/shard_map/ppermute | solution.py:214
  1522.5 84.5 %collective-permute-start.56 = (bf16[1024,1024]{1,0:T(8,128)(2,1)S(1)}, bf16[1024,1024]{1,0:T(8,128)(2,1)S(1)}, u32[]{:S(2)}, u32[]{:S(2)}) collective-permute-start(bf16[1024,1024]{1,0:T(8,128)(2,1)S(1)} %add_convert_fusion.6), channel_id=1, source_target_pairs={{0,4},{4,0},{1,5},{5,1},{2,6},{6,2},{3,7},{7,3}} | collective-permute-start | bytes 6291464 | tf_op jit(solution)/shard_map/ppermute | solution.py:214
  1530.5 121.0 %collective-permute-start.53 = (bf16[1024,1024]{1,0:T(8,128)(2,1)}, bf16[1024,1024]{1,0:T(8,128)(2,1)}, u32[]{:S(2)}, u32[]{:S(2)}) collective-permute-start(bf16[1024,1024]{1,0:T(8,128)(2,1)} %add_convert_fusion.8), channel_id=1, source_target_pairs={{0,4},{4,0},{1,5},{5,1},{2,6},{6,2},{3,7},{7,3}} | collective-permute-start | bytes 6291464 | tf_op jit(solution)/shard_map/ppermute | solution.py:214
  1612.0 55.6 %collective-permute-start.57 = (bf16[1024,1024]{1,0:T(8,128)(2,1)S(1)}, bf16[1024,1024]{1,0:T(8,128)(2,1)}, u32[]{:S(2)}, u32[]{:S(2)}) collective-permute-start(bf16[1024,1024]{1,0:T(8,128)(2,1)S(1)} %add_convert_fusion.5), channel_id=1, source_target_pairs={{0,2},{1,3},{2,0},{3,1},{4,6},{5,7},{6,4},{7,5}} | collective-permute-start | bytes 6291464 | tf_op jit(solution)/shard_map/ppermute | solution.py:205
  1656.3 47.9 %collective-permute-start.54 = (bf16[1024,1024]{1,0:T(8,128)(2,1)}, bf16[1024,1024]{1,0:T(8,128)(2,1)}, u32[]{:S(2)}, u32[]{:S(2)}) collective-permute-start(bf16[1024,1024]{1,0:T(8,128)(2,1)} %add_convert_fusion.7), channel_id=1, source_target_pairs={{0,3},{1,2},{2,1},{3,0},{4,7},{5,6},{6,5},{7,4}} | collective-permute-start | bytes 6291464 | tf_op jit(solution)/shard_map/ppermute | solution.py:205
  1666.0 47.3 %collective-permute-start.61 = (bf16[1024,1024]{1,0:T(8,128)(2,1)S(1)}, bf16[1024,1024]{1,0:T(8,128)(2,1)}, u32[]{:S(2)}, u32[]{:S(2)}) collective-permute-start(bf16[1024,1024]{1,0:T(8,128)(2,1)S(1)} %add_convert_fusion.3), channel_id=1, source_target_pairs={{0,1},{1,0},{2,3},{3,2},{4,5},{5,4},{6,7},{7,6}} | collective-permute-start | bytes 6291464 | tf_op jit(solution)/shard_map/ppermute | solution.py:202
  1667.5 99.9 %collective-permute-start.58 = (bf16[1024,1024]{1,0:T(8,128)(2,1)}, bf16[1024,1024]{1,0:T(8,128)(2,1)}, u32[]{:S(2)}, u32[]{:S(2)}) collective-permute-start(bf16[1024,1024]{1,0:T(8,128)(2,1)} %collective-permute-done.57), channel_id=1, source_target_pairs={{0,4},{4,0},{1,5},{5,1},{2,6},{6,2},{3,7},{7,3}} | collective-permute-start | bytes 6291464 | tf_op jit(solution)/shard_map/ppermute | solution.py:214
  1704.3 57.0 %collective-permute-start.55 = (bf16[1024,1024]{1,0:T(8,128)(2,1)}, bf16[1024,1024]{1,0:T(8,128)(2,1)}, u32[]{:S(2)}, u32[]{:S(2)}) collective-permute-start(bf16[1024,1024]{1,0:T(8,128)(2,1)} %collective-permute-done.54), channel_id=1, source_target_pairs={{0,4},{4,0},{1,5},{5,1},{2,6},{6,2},{3,7},{7,3}} | collective-permute-start | bytes 6291464 | tf_op jit(solution)/shard_map/ppermute | solution.py:214
  1713.3 92.9 %collective-permute-start.62 = (bf16[1024,1024]{1,0:T(8,128)(2,1)}, bf16[1024,1024]{1,0:T(8,128)(2,1)}, u32[]{:S(2)}, u32[]{:S(2)}) collective-permute-start(bf16[1024,1024]{1,0:T(8,128)(2,1)} %collective-permute-done.61), channel_id=1, source_target_pairs={{0,4},{4,0},{1,5},{5,1},{2,6},{6,2},{3,7},{7,3}} | collective-permute-start | bytes 6291464 | tf_op jit(solution)/shard_map/ppermute | solution.py:214
  1716.0 134.3 %collective-permute-start.63 = (bf16[1024,1024]{1,0:T(8,128)(2,1)}, bf16[1024,1024]{1,0:T(8,128)(2,1)}, u32[]{:S(2)}, u32[]{:S(2)}) collective-permute-start(bf16[1024,1024]{1,0:T(8,128)(2,1)} %add_convert_fusion.2), channel_id=1, source_target_pairs={{0,4},{4,0},{1,5},{5,1},{2,6},{6,2},{3,7},{7,3}} | collective-permute-start | bytes 6291464 | tf_op jit(solution)/shard_map/ppermute | solution.py:214
  1855.7 46.9 %collective-permute-start.64 = (bf16[1024,1024]{1,0:T(8,128)(2,1)}, bf16[1024,1024]{1,0:T(8,128)(2,1)S(1)}, u32[]{:S(2)}, u32[]{:S(2)}) collective-permute-start(bf16[1024,1024]{1,0:T(8,128)(2,1)} %get-tuple-element.102), channel_id=1, source_target_pairs={{0,4},{4,0},{1,5},{5,1},{2,6},{6,2},{3,7},{7,3}} | collective-permute-start | bytes 6291464 | tf_op jit(solution)/shard_map/ppermute | solution.py:214
  (69 other events, 2190.0 us)

commit v2 on v1

v2 whole, which is shorter than its diff:
```python
import jax
import jax.numpy as jnp
from jax import lax
from jax.experimental import pallas as pl
from jax.experimental.pallas import tpu as pltpu
from jax.sharding import PartitionSpec as P


EPS = 1e-6
CHUNKS = (2560, 1024, 1024, 1024, 512)
ROWS = 128
COLS = 512
SPLIT = 768
TIME_BLOCK = 256


bf16 = jnp.bfloat16
f32 = jnp.float32


def dot(a, b):
    return jnp.dot(a, b, preferred_element_type=f32)


def recurrence_kernel(u_ref, pos_ref, conv_w_ref, conv_b_ref, rate_ref, rw_ref, rb_ref, iw_ref, ib_ref, out_ref, ext, dec, drv, carry):
    rows, width = u_ref.shape
    groups = rows // 8

    @pl.when(pl.program_id(1) == 0)
    def _():
        ext[0:8, :] = jnp.zeros((8, width), f32)
        carry[...] = jnp.zeros_like(carry)

    pos = pos_ref[...]
    u = u_ref[...].astype(f32)
    ext[8:8 + rows, :] = u
    taps = conv_w_ref[...].astype(f32)
    total = conv_b_ref[...].astype(f32) + u * taps[0:1]
    for shift in range(1, conv_w_ref.shape[0]):
        total = total + jnp.where(pos >= shift, ext[8 - shift:8 - shift + rows, :], 0.0) * taps[shift:shift + 1]
    ext[0:8, :] = u[rows - 8:rows]
    conv = total.astype(bf16)
    rate = jax.nn.sigmoid(dot(conv, rw_ref[...]) + rb_ref[...].astype(f32))
    inflow = jax.nn.sigmoid(dot(conv, iw_ref[...]) + ib_ref[...].astype(f32))
    log_a = rate * rate_ref[...]
    decay = jnp.exp(log_a)
    scale = jnp.sqrt(-jnp.tanh(log_a) * (decay * decay + 1.0))
    reset = pos == 0
    decay = jnp.where(reset, 0.0, decay)
    scale = jnp.where(reset, 1.0, scale)
    drive = scale * inflow * conv.astype(f32)
    a = decay.reshape(groups, 8, width)
    b = drive.reshape(groups, 8, width)
    row = lax.broadcasted_iota(jnp.int32, (groups, 8, width), 1)
    for step in (1, 2, 4):
        keep = row >= step
        b = a * jnp.where(keep, pltpu.roll(b, step, 1), 0.0) + b
        a = a * jnp.where(keep, pltpu.roll(a, step, 1), 1.0)
    dec[...] = a
    drv[...] = b
    state = carry[0:1, :]
    for group in range(groups):
        hidden = dec[group] * state + drv[group]
        drv[group] = hidden
        state = hidden[7:8, :]
    carry[0:1, :] = state
    out_ref[...] = drv[...].reshape(rows, width)


def recurrence(u, pos, conv_w, conv_b, rate, rw, rb, iw, ib):
    tokens, width = u.shape
    blocks, block = rw.shape[0], rw.shape[1]
    time_spec = pl.BlockSpec((TIME_BLOCK, block), lambda b, t: (t, b))
    row_spec = pl.BlockSpec((1, block), lambda b, t: (0, b))
    gate_spec = pl.BlockSpec((None, block, block), lambda b, t: (b, 0, 0))
    return pl.pallas_call(
        recurrence_kernel,
        grid=(blocks, tokens // TIME_BLOCK),
        in_specs=[time_spec, pl.BlockSpec((TIME_BLOCK, 1), lambda b, t: (t, 0)),
                  pl.BlockSpec((conv_w.shape[0], block), lambda b, t: (0, b)), row_spec, row_spec,
                  gate_spec, row_spec, gate_spec, row_spec],
        out_specs=time_spec,
        out_shape=jax.ShapeDtypeStruct((tokens, width), f32),
        scratch_shapes=[pltpu.VMEM((TIME_BLOCK + 8, block), f32), pltpu.VMEM((TIME_BLOCK // 8, 8, block), f32),
                        pltpu.VMEM((TIME_BLOCK // 8, 8, block), f32), pltpu.VMEM((8, block), f32)],
        compiler_params=pltpu.CompilerParams(dimension_semantics=("arbitrary", "arbitrary")),
        cost_estimate=pl.CostEstimate(flops=tokens * width * 1200, bytes_accessed=tokens * width * 6, transcendentals=tokens * width * 8),
        name="recurrence",
    )(u, pos, conv_w, conv_b[None], rate[None], rw, rb[None], iw, ib[None])


def products(x, ws):
    depth = ws[0].shape[0]
    return sum(dot(x[:, j * depth:(j + 1) * depth], w[...]) for j, w in enumerate(ws))


def inner_kernel(low_ref, high_ref, *refs):
    gate_w, up_w, gate_b, up_b, out_ref = refs[:4], refs[4:8], refs[8], refs[9], refs[-1]
    rows = low_ref.shape[0]
    for part, m_ref in enumerate((low_ref, high_ref)):
        gate = jax.nn.gelu(products(m_ref, gate_w) + gate_b[...].astype(f32), approximate=True)
        out_ref[part * rows:(part + 1) * rows, :] = (gate * (products(m_ref, up_w) + up_b[...].astype(f32))).astype(bf16)


def inner_of(m, gate_w, up_w, gate_b, up_b, first, total, into=None):
    rows, width = m[0].shape
    depth, size = gate_w[0].shape
    tokens = 2 * rows
    weight = pl.BlockSpec((depth, COLS), lambda n: (0, n))
    vector = pl.BlockSpec((1, COLS), lambda n: (0, n))
    offset = first // COLS
    given = [] if into is None else [into]
    return pl.pallas_call(
        inner_kernel, grid=(size // COLS,),
        in_specs=[pl.BlockSpec((rows, width), lambda n: (0, 0))] * 2 + [weight] * 8 + [vector] * 2 + [pl.BlockSpec(memory_space=pl.ANY)] * len(given),
        out_specs=pl.BlockSpec((tokens, COLS), lambda n: (0, offset + n)),
        out_shape=jax.ShapeDtypeStruct((tokens, total), bf16),
        input_output_aliases={12: 0} if given else {},
        cost_estimate=pl.CostEstimate(flops=4 * tokens * width * size, bytes_accessed=4 * width * size + 2 * tokens * (width + size), transcendentals=tokens * size),
        name="inner")(*m, *gate_w, *up_w, gate_b[None], up_b[None], *given)


def project_kernel(at_ref, n_ref, *refs):
    ws, bias_ref, out_ref = refs[:4], refs[4], refs[-1]
    out_ref[...] = (products(n_ref, ws) + bias_ref[...].astype(f32)).astype(bf16)


def mix_kernel(at_ref, n_ref, *refs):
    ws, bias_ref, hidden_ref, out_ref = refs[:4], refs[4], refs[5], refs[-1]
    y = jax.nn.gelu(products(n_ref, ws) + bias_ref[...].astype(f32), approximate=True).astype(bf16)
    out_ref[...] = (hidden_ref[...] * y.astype(f32)).astype(bf16)


def project(normed, ws, bias, start, tokens, hidden=None):
    width = normed.shape[1]
    depth, size = ws[0].shape
    rows = 1024
    per = tokens // rows
    tile = pl.BlockSpec((rows, COLS), lambda i, n, at: (at[0] * per + i, n))
    given = [] if hidden is None else [hidden]
    spec = pltpu.PrefetchScalarGridSpec(
        num_scalar_prefetch=1, grid=(per, size // COLS),
        in_specs=[pl.BlockSpec((rows, width), lambda i, n, at: (at[0] * per + i, 0))] + [pl.BlockSpec((depth, COLS), lambda i, n, at: (0, n))] * 4
        + [pl.BlockSpec((1, COLS), lambda i, n, at: (0, n))] + [tile] * len(given),
        out_specs=pl.BlockSpec((rows, COLS), lambda i, n, at: (i, n)))
    return pl.pallas_call(
        project_kernel if hidden is None else mix_kernel, grid_spec=spec, out_shape=jax.ShapeDtypeStruct((tokens, size), bf16),
        cost_estimate=pl.CostEstimate(flops=2 * tokens * width * size, bytes_accessed=2 * (tokens + size) * width, transcendentals=tokens * size),
        name="project")(jnp.asarray(start, jnp.int32).reshape(1), normed, *ws, bias[None], *given)


def tie(*values):
    return lax.optimization_barrier(values)


def pick(parts, quarter):
    value = parts[0][...]
    for index in range(1, 4):
        value = jnp.where(quarter == index, parts[index][...], value)
    return value.astype(f32)


def write_norm(pieces, gain_ref, out_ref):
    width = pieces[0].shape[1]
    total = sum(jnp.sum(p * p, axis=1, keepdims=True) for p in pieces)
    inv = lax.rsqrt(total / (width * len(pieces)) + EPS)
    for j, p in enumerate(pieces):
        out_ref[:, j * width:(j + 1) * width] = (p * inv * (1.0 + gain_ref[j:j + 1, :])).astype(bf16)


def norm_kernel(at_ref, own_ref, near_ref, *refs):
    far, diag, (gain_ref, out_ref) = refs[:4], refs[4:8], refs[8:]
    quarter = (pl.program_id(0) // (pl.num_programs(0) // 4) + at_ref[0]) % 4
    pieces = [own_ref[...].astype(f32), near_ref[...].astype(f32), pick(far, quarter), pick(diag, quarter)]
    write_norm(pieces, gain_ref, out_ref)


def norm_in(shift, own, near, far, diag, gain):
    tokens, width = own.shape
    rows = 2 * ROWS
    per = tokens // rows // 4
    whole = pl.BlockSpec((rows, width), lambda i, at: (i, 0))
    parts = [pl.BlockSpec((rows, width), lambda i, at, q=q: (jnp.clip(i - (q + at[0]) % 4 * per, 0, per - 1), 0)) for q in range(4)]
    spec = pltpu.PrefetchScalarGridSpec(
        num_scalar_prefetch=1, grid=(tokens // rows,),
        in_specs=[whole, whole] + parts + parts + [pl.BlockSpec((4, width), lambda i, at: (0, 0))],
        out_specs=pl.BlockSpec((rows, 4 * width), lambda i, at: (i, 0)))
    return pl.pallas_call(
        norm_kernel, grid_spec=spec, out_shape=jax.ShapeDtypeStruct((tokens, 4 * width), bf16),
        cost_estimate=pl.CostEstimate(flops=tokens * width * 600, bytes_accessed=tokens * width * 16, transcendentals=0),
        name="norm_in")(shift, own, near, *far, *diag, gain)


def resid_kernel(at_ref, own_ref, near_ref, *refs):
    far, diag, kept, got = refs[:4], refs[4:8], refs[8:12], refs[12:16]
    bias_ref, gain_ref = refs[16:18]
    out, norm_ref = refs[-5:-1], refs[-1]
    quarter = at_ref[2]
    base = [own_ref[...].astype(f32), near_ref[...].astype(f32), pick(far, quarter), pick(diag, quarter)]
    pieces = [b + (k[...] + g[...].astype(f32)) + bias_ref[j:j + 1, :] for j, (b, k, g) in enumerate(zip(base, kept, got))]
    for o, p in zip(out, pieces):
        o[...] = p
    write_norm(pieces, gain_ref, norm_ref)


def resid_norm(at, part, own, near, far, diag, kept, got, bias, gain, into=()):
    rows, width = got[0].shape
    tokens = kept[0].shape[0]
    all_blocks, per = tokens // ROWS, rows // ROWS
    base = part * per

    def at_row(k):
        return pl.BlockSpec((ROWS, width), lambda i, at: (at[k] * all_blocks + base + i, 0))

    here = pl.BlockSpec((ROWS, width), lambda i, at: (base + i, 0))
    whole = pl.BlockSpec((ROWS, width), lambda i, at: (i, 0))
    parts = [pl.BlockSpec((ROWS, width), lambda i, at, q=q: (jnp.where(at[2] == q, base + i, 0), 0)) for q in range(4)]
    vector = pl.BlockSpec((4, width), lambda i, at: (0, 0))
    spec = pltpu.PrefetchScalarGridSpec(
        num_scalar_prefetch=1, grid=(per,),
        in_specs=[at_row(0), at_row(1)] + parts + parts + [here] * 4 + [whole] * 4 + [vector] * 2 + [pl.BlockSpec(memory_space=pl.ANY)] * len(into),
        out_specs=[here] * 4 + [pl.BlockSpec((ROWS, 4 * width), lambda i, at: (i, 0))])
    shape = jax.ShapeDtypeStruct((tokens, width), f32)
    out = pl.pallas_call(
        resid_kernel, grid_spec=spec, out_shape=[shape] * 4 + [jax.ShapeDtypeStruct((rows, 4 * width), bf16)],
        input_output_aliases={21 + j: j for j in range(len(into))},
        cost_estimate=pl.CostEstimate(flops=rows * width * 1600, bytes_accessed=rows * width * 40, transcendentals=0),
        name="resid_norm")(at, own, near, *far, *diag, *kept, *got, bias, gain, *into)
    return out[:4], out[4]


def solution(mesh):
    row_spec = P('dp', 'wd')
    specs = (row_spec, P('dp', None), P('wd'), P('wd', 'ch'), P('ch'), P('wd', 'ch'), P('ch'), P(None, 'ch'), P('ch'), P('ch'), P('ch', None, None), P('ch'), P('ch', None, None), P('ch'), P('ch', 'wd'), P('wd'), P('wd'), P('wd', 'ch'), P('ch'), P('wd', 'ch'), P('ch'), P('ch', 'wd'), P('wd'))

    def pc(a):
        return lax.ppermute(a, 'wd', [(i, i ^ 1) for i in range(4)])

    def over_x(a, flip):
        return lax.ppermute(a, 'wd', [(i, i ^ flip) for i in range(4)])

    def px(a):
        return over_x(a, 2)

    def pd(a):
        return over_x(a, 3)

    def py(a):
        return lax.ppermute(a, 'ch', [(0, 1), (1, 0)])

    def local_layer(resid_in, seg_pos, gain_temporal, w_x, bias_x, w_y, bias_y, conv_w, conv_bias, lam_param, rgate_w, rgate_b, igate_w, igate_b, w_o, bias_o, gain_mlp, w_g, bias_g, w_u, bias_u, w_d, bias_d):
        tokens, local_width = resid_in.shape
        _, steps = seg_pos.shape
        half, quarter = steps // 2, steps // 4
        wd = lax.axis_index('wd')
        cy = lax.axis_index('ch')
        cx, core = wd // 2, wd % 2
        blocks, block = rgate_w.shape[0], rgate_w.shape[1]
        my_blocks = (blocks + 1) // 2
        first_block = core * (blocks - my_blocks)
        other_block = (1 - core) * (blocks - my_blocks)
        lanes = my_blocks * block

        def rows(a, start, size):
            return lax.dynamic_slice_in_dim(a, start, size, axis=0)

        def cols(a, start, size):
            return lax.dynamic_slice_in_dim(a, start, size, axis=a.ndim - 1)

        def my_cols(w):
            return cols(w, first_block * block, lanes)

        x_first = [rows(resid_in, (1 - cx) * steps + cy * half + c * quarter, quarter) for c in range(2)]
        far_mine = [px(a) for a in x_first]
        vec = jnp.stack([gain_temporal, gain_mlp, bias_o, bias_d])
        vecs = [vec, pc(vec), px(vec), pd(vec)]
        x_own = rows(resid_in, cx * steps, steps)
        x_near = pc(x_own)
        shares = []
        for w in (w_x, w_y):
            mine, others = my_cols(w), cols(w, other_block * block, lanes)
            shares.append((mine, pc(others), px(mine), pd(others)))
        wo_far = px(w_o)
        bounds = [sum(CHUNKS[:c]) for c in range(len(CHUNKS) + 1)]
        chunk = [slice(lo, hi) for lo, hi in zip(bounds, bounds[1:])]
        gates = [(w, pc(w), px(w)) for part in chunk for w in (w_g[:, part], w_u[:, part])]
        split = SPLIT
        sides = [slice(0, split), slice(split, local_width)]
        d_near = pc(w_d)
        d_far = [px(w_d[:, part]) for part in sides]

        table = jnp.stack([v.astype(f32) for v in vecs], axis=1)
        gain_t, gain_m, b_o, b_d = table[0], table[1], table[2], table[3]

        far_other = [py(a) for a in far_mine]
        far = far_mine + far_other
        diag = [pc(a) for a in far]
        shift = (2 * cy).astype(jnp.int32).reshape(1)
        normed = norm_in(shift, x_own, x_near, far, diag, gain_t)

        u = project(normed, shares[0], my_cols(bias_x), 0, steps)
        rate = -8.0 * jax.nn.softplus(-my_cols(lam_param))
        pos = rows(seg_pos, cx, 1).reshape(steps, 1)
        hidden = recurrence(u, pos, my_cols(conv_w), my_cols(conv_bias), rate,
                            rows(rgate_w, first_block, my_blocks), my_cols(rgate_b),
                            rows(igate_w, first_block, my_blocks), my_cols(igate_b))
        hidden, *wy = tie(hidden, *shares[1])
        given = project(normed, wy, my_cols(bias_y), 1 - core, half, hidden)
        given, hidden = tie(given, hidden)
        got = pc(given)
        kept = project(normed, wy, my_cols(bias_y), core, half, hidden)

        first = core == 0
        mixed_all = jnp.concatenate([jnp.where(first, kept, got), jnp.where(first, got, kept)[:, 2 * lanes - blocks * block:]], axis=1)
        wo = [w_o, pc(w_o)]
        mixed_send = rows(mixed_all, (1 - cy) * quarter, quarter)
        mixed_keep = rows(mixed_all, cy * quarter, quarter)
        cut = quarter // 2
        received = [[None] * 4, [None] * 4]

        def send_part(r, j):
            part = dot(mixed_send[r * cut:(r + 1) * cut], wo[j]).astype(bf16)
            received[r][j] = py(part)
            return part

        ready = [send_part(0, j) for j in (0, 1)]
        mixed_keep, mixed_send, wo_far, *_ = tie(mixed_keep, mixed_send, wo_far, *ready)
        wo += [wo_far, pc(wo_far)]
        for r, j in ((0, 2), (0, 3), (1, 0), (1, 1), (1, 2), (1, 3)):
            send_part(r, j)
        own = [dot(mixed_keep, w) for w in wo]
        my_quarter = core * 2 + cy
        at = jnp.stack([cx * 4 + my_quarter, my_quarter, (my_quarter + 2 * cy) % 4]).astype(jnp.int32)
        m_own, resid = [None] * 2, ()
        for r in range(2):
            resid, m_own[r] = resid_norm(at, r, resid_in, x_near, far, diag, own, received[r], b_o, gain_m, resid)
        m_other = [py(m) for m in m_own]

        def relay(w, far_piece):
            return [w[0], w[1], far_piece, pc(far_piece)]

        def up(m, c, ws, into=None):
            return inner_of(m, ws[0], ws[1], bias_g[chunk[c]], bias_u[chunk[c]], bounds[c], bounds[-1], into)

        def arrive(c, *values):
            *values, far_g, far_u = tie(*values, gates[2 * c][2], gates[2 * c + 1][2])
            return values, (relay(gates[2 * c], far_g), relay(gates[2 * c + 1], far_u))

        m_own, w0 = arrive(0, *m_own)
        inner_own = up(m_own, 0, w0)
        (inner_own,), w1 = arrive(1, inner_own)
        inner_own = up(m_own, 1, w1, inner_own)
        inner_own, *m_other = tie(inner_own, *m_other)
        inner_other = up(m_other, 0, w0)
        inner_other = up(m_other, 1, w1, inner_other)
        for c in (2, 3):
            (inner_other, inner_own), ws = arrive(c, inner_other, inner_own)
            inner_other = up(m_other, c, ws, inner_other)
            inner_own, inner_other = tie(inner_own, inner_other)
            inner_own = up(m_own, c, ws, inner_own)
        (inner_other, inner_own), ws = arrive(4, inner_other, inner_own)
        inner_other = up(m_other, 4, ws, inner_other)

        hops = (lambda a: a, pc, lambda a: over_x(a, 2), lambda a: over_x(a, 3))
        pieces = []
        whole = slice(0, local_width)

        def part(w):
            return dot(inner_other, w).astype(bf16)

        def finish(j, h, mine, down):
            at = (whole,) + tuple(sides)
            return (resid[j][:, at[h]] + (mine + down.astype(f32)) + b_d[j, at[h]]).astype(bf16)

        def hand_on(j, h, out):
            moved = hops[j](out)
            pieces.append((j, (0, 0, split)[h], moved, py(moved)))

        near = [w_d, d_near]
        part1 = part(near[1])
        sum1 = py(part1)
        part0 = part(near[0])
        sum0 = py(part0)
        inner_own, *_ = tie(inner_own, part0, part1)
        inner_own = up(m_own, 4, ws, inner_own)
        out1 = finish(1, 0, dot(inner_own, near[1]), sum1)
        hand_on(1, 0, out1)
        out0 = finish(0, 0, dot(inner_own, near[0]), sum0)
        hand_on(0, 0, out0)
        result = jnp.zeros((tokens, local_width), bf16)
        near_mine = pieces[0][2]
        result = lax.dynamic_update_slice(result, near_mine, (jnp.bitwise_xor(wd, 1) * half + cy * quarter, 0))
        inner_own, inner_other, far_a, *_ = tie(inner_own, inner_other, d_far[0], out0, out1)
        d = [far_a, pc(far_a)]
        parts_a = [part(d[j]) for j in range(2)]
        sums_a = [py(v) for v in parts_a]
        inner_own, *_ = tie(inner_own, *parts_a)
        mine2a = dot(inner_own, d[0])
        mine3a = dot(inner_own, d[1])
        mine_a = tie(mine2a, mine3a)
        out2a = finish(2, 1, mine_a[0], sums_a[0])
        hand_on(2, 1, out2a)
        inner_own, inner_other, far_b, mine3a, _ = tie(inner_own, inner_other, d_far[1], mine_a[1], out2a)
        d = [far_b, pc(far_b)]
        parts_b = [part(d[j]) for j in range(2)]
        sums_b = [py(v) for v in parts_b]
        hand_on(3, 1, finish(3, 1, mine3a, sums_a[1]))
        inner_own, *_ = tie(inner_own, *parts_b)
        mine_b = tie(*[dot(inner_own, w) for w in d])
        for j in range(2):
            hand_on(j + 2, 2, finish(j + 2, 2, mine_b[j], sums_b[j]))
        near_other, own_mine, own_other, _ = tie(pieces[0][3], pieces[1][2], pieces[1][3], mine_b[0])
        pieces[:2] = [(1, 0, near_mine, near_other), (0, 0, own_mine, own_other)]

        for j, col, mine, other in pieces:
            base = jnp.bitwise_xor(wd, j) * half
            for value, row in ((mine, base + cy * quarter), (other, base + (1 - cy) * quarter)):
                if value is not near_mine:
                    result = lax.dynamic_update_slice(result, value, (row, col))
        return result

    return jax.shard_map(local_layer, mesh=mesh, in_specs=specs, out_specs=row_spec, check_vma=False)
```

time: 1910 us -> 1800 us (0.942)
  matrix products: 389 us -> 234 us
  Pallas kernels: 420 us -> 573 us
  waiting for transfers between devices: 881 us -> 797 us
  other arithmetic: 64.9 us -> 31.5 us
    dot_general x34 -> x24, matrix products: 389 us -> 234 us  [dot(): return jnp.dot(a, b, preferred_element_type=f32)]
    pallas_call x0 -> x3, Pallas kernels: none -> 137 us  [project(): pl.pallas_call(project_kernel if hidden is None else mix_kernel, grid_spe...]
    ppermute x20 -> x25, waiting for transfers between devices: 464 us -> 418 us  [over_x(): return lax.ppermute(a, 'wd', [(i, i ^ flip) for i in range(4)])]
    ppermute x15 -> x24, waiting for transfers between devices: 397 us -> 371 us  [py(): return lax.ppermute(a, 'ch', [(0, 1), (1, 0)])]
    pallas_call x6 -> x10, Pallas kernels: 278 us -> 294 us  [inner_of(): pl.pallas_call(inner_kernel, grid=(size // COLS,), in_specs=[pl.BlockSpec...]
  transfers between devices with their start and end apart: 65 -> 84, of which waited for: 24 -> 31; matrix products, arithmetic and copies ran while one was open for 28% -> 20% of each run, Pallas kernels for 22% -> 30%
where the time goes in v2:
time: 1800 us; the launch traced here: 1790 us
  waiting for transfers between devices  797 us (44%)
  Pallas kernels  573 us (32%)
  matrix products  234 us (13%)
  local copies, waits for them, and re-layouts  95.9 us (5%)
  starting transfers between devices  62 us (3%)
  other arithmetic  31.5 us (2%)
    ppermute x25, waiting for transfers between devices, over_x(): return lax.ppermute(a, 'wd', [(i, i ^ flip) for i in range(4)])  418 us
    ppermute x24, waiting for transfers between devices, py(): return lax.ppermute(a, 'ch', [(0, 1), (1, 0)])  371 us
    pallas_call x10, Pallas kernels, inner_of(): pl.pallas_call(inner_kernel, grid=(size // COLS,), in_specs=[pl.BlockSpec...  294 us
    dot_general x24, matrix products, dot(): return jnp.dot(a, b, preferred_element_type=f32)  234 us
    pallas_call x3, Pallas kernels, project(): pl.pallas_call(project_kernel if hidden is None else mix_kernel, grid_spe...  137 us
    pallas_call x1, Pallas kernels, recurrence(): pl.pallas_call(recurrence_kernel, grid=(blocks, tokens // TIME_BLOCK), in...  88.2 us
  transfers between devices with their start and end apart: 84, of which 31 were waited for; matrix products, arithmetic and copies ran while one was open for 20% of the time, Pallas kernels for 30%

profile of v2, /device:TPU:0, one launch (start us, length us, event | category | flops | bytes accessed | tf_op | source)
XLA Modules:
  0.0 1793.4 jit_solution(9630564224518719698)
XLA Ops:
  7.9 7.9 constant_dynamic-slice_fusion.9.own_ref
  15.9 38.7 %collective-permute-done.1.refs_0_ = bf16[1024,1024]{1,0:T(8,128)(2,1)S(1)} collective-permute-done((bf16[1024,1024]{1,0:T(8,128)(2,1)}, bf16[1024,1024]{1,0:T(8,128)(2,1)S(1)}, u32[]{:S(2)}, u32[]{:S(2)}) %collective-permute-start.1) | collective-permute-done | bytes 2097184 | tf_op jit(solution)/shard_map/ppermute | solution.py:240
  59.2 39.8 %collective-permute-done.2.refs_1_ = bf16[1024,1024]{1,0:T(8,128)(2,1)} collective-permute-done((bf16[1024,1024]{1,0:T(8,128)(2,1)S(1)}, bf16[1024,1024]{1,0:T(8,128)(2,1)}, u32[]{:S(2)}, u32[]{:S(2)}) %collective-permute-start.2) | collective-permute-done | bytes 2097184 | tf_op jit(solution)/shard_map/ppermute | solution.py:240
  101.3 5.9 constant_dynamic-slice_fusion.5
  107.3 38.6 %collective-permute-done.4.refs_3_ = bf16[1024,1024]{1,0:T(8,128)(2,1)} collective-permute-done((bf16[1024,1024]{1,0:T(8,128)(2,1)}, bf16[1024,1024]{1,0:T(8,128)(2,1)}, u32[]{:S(2)}, u32[]{:S(2)}) %collective-permute-start.4) | collective-permute-done | bytes 2097184 | tf_op jit(solution)/shard_map/ppermute | solution.py:249
  157.6 5.9 constant_dynamic-slice_fusion
  165.9 30.5 %norm_in.1.n_ref = bf16[4096,4096]{1,0:T(8,128)(2,1)} custom-call(s32[1]{0:T(128)} %bitcast.4.at_ref, bf16[4096,1024]{1,0:T(8,128)(2,1)} %constant_dynamic-slice_fusion.9.own_ref, bf16[4096,1024]{1,0:T(8,128)(2,1)} %collective-permute-done.near_ref, bf16[1024,1024]{1,0:T(8,128)(2,1)} %copy-done.2, bf16[1024,1024]{1,0:T(8,128)(2,1)} %collective-permute-done.2.refs_1_, ...), custom_call_target="tpu_custom_call" | custom-call | flops 2516582400 | bytes 67108864 | tf_op jit(solution)/shard_map/norm_in/pallas_call | solution.py:188
  197.7 19.5 %collective-permute-done.13.refs_2_ = bf16[1024,1536]{1,0:T(8,128)(2,1)} collective-permute-done((bf16[1024,1536]{1,0:T(8,128)(2,1)}, bf16[1024,1536]{1,0:T(8,128)(2,1)}, u32[]{:S(2)}, u32[]{:S(2)}) %collective-permute-start.13) | collective-permute-done | bytes 3145760 | tf_op jit(solution)/shard_map/ppermute | solution.py:240
  217.2 66.5 %collective-permute-done.14.refs_3_ = bf16[1024,1536]{1,0:T(8,128)(2,1)} collective-permute-done((bf16[1024,1536]{1,0:T(8,128)(2,1)}, bf16[1024,1536]{1,0:T(8,128)(2,1)}, u32[]{:S(2)}, u32[]{:S(2)}) %collective-permute-start.14) | collective-permute-done | bytes 3145760 | tf_op jit(solution)/shard_map/ppermute | solution.py:240
  283.7 61.0 %project.3.u_ref = bf16[4096,1536]{1,0:T(8,128)(2,1)} custom-call(s32[1]{0:T(128)} %constant.69.clone.1.at_ref, bf16[4096,4096]{1,0:T(8,128)(2,1)} %norm_in.1.n_ref, bf16[1024,1536]{1,0:T(8,128)(2,1)} %get-tuple-element.146.refs_0_, bf16[1024,1536]{1,0:T(8,128)(2,1)} %collective-permute-done.12.refs_1_, bf16[1024,1536]{1,0:T(8,128)(2,1)} %collective-permute-done.13.refs_2_, ...), custom_call_target="tpu_custom_call" | custom-call | flops 51539607552 | bytes 46137344 | tf_op jit(solution)/shard_map/project/pallas_call | solution.py:146
  344.7 88.2 %recurrence.1.refs_5_ = f32[4096,1536]{1,0:T(8,128)} custom-call(bf16[4096,1536]{1,0:T(8,128)(2,1)} %project.3.u_ref, s32[4096,1]{1,0:T(8,128)} %copy.40.pos_ref, bf16[4,1536]{1,0:T(4,128)(2,1)} %constant_dynamic-slice_fusion.4.conv_w_ref, bf16[1,1536]{1,0:T(2,128)(2,1)} %broadcast_in_dim.64.conv_b_ref, f32[1,1536]{1,0:T(1,128)} %broadcast_in_dim.65.rate_ref, ...), custom_call_target="tpu_custom_call" | custom-call | flops 7549747200 | bytes 37748736 | tf_op jit(solution)/shard_map/recurrence/pallas_call | solution.py:76
  434.6 37.8 %project.4 = bf16[2048,1536]{1,0:T(8,128)(2,1)} custom-call(s32[1]{0:T(128)} %bitcast.9.at_ref, bf16[4096,4096]{1,0:T(8,128)(2,1)} %norm_in.1.n_ref, bf16[1024,1536]{1,0:T(8,128)(2,1)} %get-tuple-element.68.refs_0_, bf16[1024,1536]{1,0:T(8,128)(2,1)} %collective-permute-done.15.refs_1_, bf16[1024,1536]{1,0:T(8,128)(2,1)} %copy-done.42, ...), custom_call_target="tpu_custom_call" | custom-call | flops 25769803776 | bytes 29360128 | tf_op jit(solution)/shard_map/project/pallas_call | solution.py:146
  488.1 38.0 %project.5 = bf16[2048,1536]{1,0:T(8,128)(2,1)} custom-call(s32[1]{0:T(128)} %bitcast.3.at_ref, bf16[4096,4096]{1,0:T(8,128)(2,1)} %norm_in.1.n_ref, bf16[1024,1536]{1,0:T(8,128)(2,1)} %get-tuple-element.68.refs_0_, bf16[1024,1536]{1,0:T(8,128)(2,1)} %collective-permute-done.15.refs_1_, bf16[1024,1536]{1,0:T(8,128)(2,1)} %copy-done.42, ...), custom_call_target="tpu_custom_call" | custom-call | flops 25769803776 | bytes 29360128 | tf_op jit(solution)/shard_map/project/pallas_call | solution.py:146
  526.1 6.9 slice_select_fusion
  540.3 6.0 fusion.39
  551.0 50.0 %collective-permute-done.19 = bf16[2816,1024]{1,0:T(8,128)(2,1)} collective-permute-done((bf16[2816,1024]{1,0:T(8,128)(2,1)}, bf16[2816,1024]{1,0:T(8,128)(2,1)}, u32[]{:S(2)}, u32[]{:S(2)}) %collective-permute-start.19) | collective-permute-done | bytes 5767200 | tf_op jit(solution)/shard_map/ppermute | solution.py:240
  608.4 9.5 fusion.50.refs_10_
  623.7 8.0 fusion.48.refs_8_
  631.7 9.5 fusion.49.refs_9_
  651.1 6.9 fusion.21
  662.1 9.3 collective-permute-done.26.refs_12_
  671.9 21.9 %collective-permute-done.24.refs_14_ = bf16[512,1024]{1,0:T(8,128)(2,1)S(1)} collective-permute-done((bf16[512,1024]{1,0:T(8,128)(2,1)S(1)}, bf16[512,1024]{1,0:T(8,128)(2,1)S(1)}, u32[]{:S(2)}, u32[]{:S(2)}) %collective-permute-start.24) | collective-permute-done | bytes 1048608 | tf_op jit(solution)/shard_map/ppermute | solution.py:249
  694.4 22.0 %collective-permute-done.29.refs_15_ = bf16[512,1024]{1,0:T(8,128)(2,1)} collective-permute-done((bf16[512,1024]{1,0:T(8,128)(2,1)S(1)}, bf16[512,1024]{1,0:T(8,128)(2,1)}, u32[]{:S(2)}, u32[]{:S(2)}) %collective-permute-start.29) | collective-permute-done | bytes 1048608 | tf_op jit(solution)/shard_map/ppermute | solution.py:249
  717.0 7.9 fusion.51.refs_11_
  724.9 11.7 resid_norm.2
  738.8 22.5 %collective-permute-done.22.refs_12_ = bf16[512,1024]{1,0:T(8,128)(2,1)S(1)} collective-permute-done((bf16[512,1024]{1,0:T(8,128)(2,1)}, bf16[512,1024]{1,0:T(8,128)(2,1)S(1)}, u32[]{:S(2)}, u32[]{:S(2)}) %collective-permute-start.22) | collective-permute-done | bytes 1048608 | tf_op jit(solution)/shard_map/ppermute | solution.py:249
  761.3 21.8 %collective-permute-done.25.refs_15_ = bf16[512,1024]{1,0:T(8,128)(2,1)} collective-permute-done((bf16[512,1024]{1,0:T(8,128)(2,1)}, bf16[512,1024]{1,0:T(8,128)(2,1)}, u32[]{:S(2)}, u32[]{:S(2)}) %collective-permute-start.25) | collective-permute-done | bytes 1048608 | tf_op jit(solution)/shard_map/ppermute | solution.py:249
  783.1 11.7 resid_norm.3
  794.9 30.3 %collective-permute-done.31.refs_6_ = bf16[1024,2560]{1,0:T(8,128)(2,1)} collective-permute-done((bf16[1024,2560]{1,0:T(8,128)(2,1)}, bf16[1024,2560]{1,0:T(8,128)(2,1)}, u32[]{:S(2)}, u32[]{:S(2)}) %collective-permute-start.31) | collective-permute-done | bytes 5242912 | tf_op jit(solution)/shard_map/ppermute | solution.py:240
  843.2 52.9 %inner.10.refs_10_ = bf16[1024,6144]{1,0:T(8,128)(2,1)} custom-call(bf16[512,4096]{1,0:T(8,128)(2,1)} %get-tuple-element.85.low_ref, bf16[512,4096]{1,0:T(8,128)(2,1)} %get-tuple-element.86.high_ref, bf16[1024,2560]{1,0:T(8,128)(2,1)} %slice.149.refs_0_, bf16[1024,2560]{1,0:T(8,128)(2,1)} %collective-permute-done.34.refs_1_, ...), custom_call_target="tpu_custom_call" | custom-call | flops 42949672960 | bytes 55574528 | tf_op jit(solution)/shard_map/inner/pallas_call | solution.py:113
  896.1 28.0 %collective-permute-done.39.refs_6_ = bf16[1024,1024]{1,0:T(8,128)(2,1)} collective-permute-done((bf16[1024,1024]{1,0:T(8,128)(2,1)}, bf16[1024,1024]{1,0:T(8,128)(2,1)}, u32[]{:S(2)}, u32[]{:S(2)}) %collective-permute-start.39) | collective-permute-done | bytes 2097184 | tf_op jit(solution)/shard_map/ppermute | solution.py:240
  934.3 26.0 %inner.11.refs_10_ = bf16[1024,6144]{1,0:T(8,128)(2,1)} custom-call(bf16[512,4096]{1,0:T(8,128)(2,1)} %get-tuple-element.85.low_ref, bf16[512,4096]{1,0:T(8,128)(2,1)} %get-tuple-element.86.high_ref, bf16[1024,1024]{1,0:T(8,128)(2,1)} %get-tuple-element.139.refs_0_, ...), custom_call_target="tpu_custom_call", output_to_operand_aliasing={{}: (12, {})} | custom-call | flops 17179869184 | bytes 27262976 | tf_op jit(solution)/shard_map/inner/pallas_call | solution.py:113
  960.3 63.1 %collective-permute-done.43.low_ref = bf16[512,4096]{1,0:T(8,128)(2,1)} collective-permute-done((bf16[512,4096]{1,0:T(8,128)(2,1)}, bf16[512,4096]{1,0:T(8,128)(2,1)}, u32[]{:S(2)}, u32[]{:S(2)}) %collective-permute-start.43) | collective-permute-done | bytes 4194336 | tf_op jit(solution)/shard_map/ppermute | solution.py:249
  1023.4 53.0 %inner.12.refs_10_ = bf16[1024,6144]{1,0:T(8,128)(2,1)} custom-call(bf16[512,4096]{1,0:T(8,128)(2,1)} %collective-permute-done.43.low_ref, bf16[512,4096]{1,0:T(8,128)(2,1)} %collective-permute-done.44.high_ref, bf16[1024,2560]{1,0:T(8,128)(2,1)} %slice.149.refs_0_, bf16[1024,2560]{1,0:T(8,128)(2,1)} %collective-permute-done.34.refs_1_, ...), custom_call_target="tpu_custom_call" | custom-call | flops 42949672960 | bytes 55574528 | tf_op jit(solution)/shard_map/inner/pallas_call | solution.py:113
  1076.4 26.4 %inner.13.refs_10_ = bf16[1024,6144]{1,0:T(8,128)(2,1)} custom-call(bf16[512,4096]{1,0:T(8,128)(2,1)} %collective-permute-done.43.low_ref, bf16[512,4096]{1,0:T(8,128)(2,1)} %collective-permute-done.44.high_ref, bf16[1024,1024]{1,0:T(8,128)(2,1)} %get-tuple-element.139.refs_0_, ...), custom_call_target="tpu_custom_call", output_to_operand_aliasing={{}: (12, {})} | custom-call | flops 17179869184 | bytes 27262976 | tf_op jit(solution)/shard_map/inner/pallas_call | solution.py:113
  1110.5 25.9 %inner.14.refs_10_ = bf16[1024,6144]{1,0:T(8,128)(2,1)} custom-call(bf16[512,4096]{1,0:T(8,128)(2,1)} %collective-permute-done.43.low_ref, bf16[512,4096]{1,0:T(8,128)(2,1)} %collective-permute-done.44.high_ref, bf16[1024,1024]{1,0:T(8,128)(2,1)} %copy-done.15, bf16[1024,1024]{1,0:T(8,128)(2,1)} %collective-permute-done.47.refs_1_, ...), custom_call_target="tpu_custom_call", output_to_operand_aliasing={{}: (12, {})} | custom-call | flops 17179869184 | bytes 27262976 | tf_op jit(solution)/shard_map/inner/pallas_call | solution.py:113
  1136.4 26.0 %inner.15.refs_10_ = bf16[1024,6144]{1,0:T(8,128)(2,1)} custom-call(bf16[512,4096]{1,0:T(8,128)(2,1)} %get-tuple-element.85.low_ref, bf16[512,4096]{1,0:T(8,128)(2,1)} %get-tuple-element.86.high_ref, bf16[1024,1024]{1,0:T(8,128)(2,1)} %copy-done.15, bf16[1024,1024]{1,0:T(8,128)(2,1)} %collective-permute-done.47.refs_1_, ...), custom_call_target="tpu_custom_call", output_to_operand_aliasing={{}: (12, {})} | custom-call | flops 17179869184 | bytes 27262976 | tf_op jit(solution)/shard_map/inner/pallas_call | solution.py:113
  1162.4 33.8 %collective-permute-done.52.refs_6_ = bf16[1024,1024]{1,0:T(8,128)(2,1)} collective-permute-done((bf16[1024,1024]{1,0:T(8,128)(2,1)}, bf16[1024,1024]{1,0:T(8,128)(2,1)}, u32[]{:S(2)}, u32[]{:S(2)}) %collective-permute-start.52) | collective-permute-done | bytes 2097184 | tf_op jit(solution)/shard_map/ppermute | solution.py:240
  1205.5 26.1 %inner.16.refs_10_ = bf16[1024,6144]{1,0:T(8,128)(2,1)} custom-call(bf16[512,4096]{1,0:T(8,128)(2,1)} %collective-permute-done.43.low_ref, bf16[512,4096]{1,0:T(8,128)(2,1)} %collective-permute-done.44.high_ref, bf16[1024,1024]{1,0:T(8,128)(2,1)} %get-tuple-element.138.refs_0_, ...), custom_call_target="tpu_custom_call", output_to_operand_aliasing={{}: (12, {})} | custom-call | flops 17179869184 | bytes 27262976 | tf_op jit(solution)/shard_map/inner/pallas_call | solution.py:113
  1231.6 26.2 %inner.17.refs_10_ = bf16[1024,6144]{1,0:T(8,128)(2,1)} custom-call(bf16[512,4096]{1,0:T(8,128)(2,1)} %get-tuple-element.85.low_ref, bf16[512,4096]{1,0:T(8,128)(2,1)} %get-tuple-element.86.high_ref, bf16[1024,1024]{1,0:T(8,128)(2,1)} %get-tuple-element.138.refs_0_, ...), custom_call_target="tpu_custom_call", output_to_operand_aliasing={{}: (12, {})} | custom-call | flops 17179869184 | bytes 27262976 | tf_op jit(solution)/shard_map/inner/pallas_call | solution.py:113
  1258.4 7.8 slice.171
  1268.3 15.7 inner.18
  1284.0 18.8 %convolution_convert_fusion.1 = bf16[1024,1024]{1,0:T(8,128)(2,1)} fusion(bf16[1024,6144]{1,0:T(8,128)(2,1)} %inner.18, bf16[6144,1024]{1,0:T(8,128)(2,1)} %param.44), kind=kOutput, calls=%fused_computation.21 | convolution fusion | flops 12885950464 | bytes 27262976 | tf_op jit(solution)/shard_map/dot_general | solution.py:22
  1304.4 16.7 convolution_convert_fusion
  1321.6 15.6 inner.19
  1337.2 19.4 %fusion.53 = f32[1024,1024]{1,0:T(8,128)} fusion(bf16[1024,6144]{1,0:T(8,128)(2,1)} %inner.19, bf16[6144,1024]{1,0:T(8,128)(2,1)} %param.44), kind=kOutput, calls=%fused_computation.91 | convolution fusion | flops 12884901888 | bytes 29360128 | tf_op jit(solution)/shard_map/dot_general | solution.py:22
  1356.6 16.2 fusion.52
  1378.6 17.1 collective-permute-done.63
  1398.2 74.4 %collective-permute-done.68 = bf16[6144,768]{1,0:T(8,128)(2,1)} collective-permute-done((bf16[6144,768]{1,0:T(8,128)(2,1)}, bf16[6144,768]{1,0:T(8,128)(2,1)}, u32[]{:S(2)}, u32[]{:S(2)}) %collective-permute-start.68) | collective-permute-done | bytes 9437216 | tf_op jit(solution)/shard_map/ppermute | solution.py:240
  1476.2 14.9 convolution_convert_fusion.3
  1492.7 15.6 convolution_convert_fusion.2
  1508.3 13.2 fusion.54
  1521.5 12.6 fusion.55
  1538.1 7.3 collective-permute-done.70
  1554.3 9.7 convolution_convert_fusion.5
  1564.0 18.8 %collective-permute-done.75 = bf16[1024,768]{1,0:T(8,128)(2,1)S(1)} collective-permute-done((bf16[1024,768]{1,0:T(8,128)(2,1)}, bf16[1024,768]{1,0:T(8,128)(2,1)S(1)}, u32[]{:S(2)}, u32[]{:S(2)}) %collective-permute-start.75) | collective-permute-done | bytes 1572896 | tf_op jit(solution)/shard_map/ppermute | solution.py:249
  1589.9 9.8 convolution_convert_fusion.4
  1599.8 6.3 fusion.56
  1606.1 20.0 %collective-permute-done.76 = bf16[1024,768]{1,0:T(8,128)(2,1)S(1)} collective-permute-done((bf16[1024,768]{1,0:T(8,128)(2,1)}, bf16[1024,768]{1,0:T(8,128)(2,1)S(1)}, u32[]{:S(2)}, u32[]{:S(2)}) %collective-permute-start.76) | collective-permute-done | bytes 1572896 | tf_op jit(solution)/shard_map/ppermute | solution.py:240
  1626.6 6.3 fusion.57
  1632.9 51.2 %collective-permute-done.78 = bf16[1024,256]{1,0:T(8,128)(2,1)} collective-permute-done((bf16[1024,256]{1,0:T(8,128)(2,1)}, bf16[1024,256]{1,0:T(8,128)(2,1)}, u32[]{:S(2)}, u32[]{:S(2)}) %collective-permute-start.78) | collective-permute-done | bytes 524320 | tf_op jit(solution)/shard_map/ppermute | solution.py:249
  1692.6 69.6 %collective-permute-done.81 = bf16[1024,256]{1,0:T(8,128)(2,1)S(1)} collective-permute-done((bf16[1024,256]{1,0:T(8,128)(2,1)}, bf16[1024,256]{1,0:T(8,128)(2,1)S(1)}, u32[]{:S(2)}, u32[]{:S(2)}) %collective-permute-start.81) | collective-permute-done | bytes 524320 | tf_op jit(solution)/shard_map/ppermute | solution.py:249
  1769.8 6.7 collective-permute-done.82
  1781.4 11.0 collective-permute-done.83
  (344 shorter events, 195.8 us)
Async XLA Ops:
  4.6 50.0 %collective-permute-start.1 = (bf16[1024,1024]{1,0:T(8,128)(2,1)}, bf16[1024,1024]{1,0:T(8,128)(2,1)S(1)}, u32[]{:S(2)}, u32[]{:S(2)}) collective-permute-start(bf16[1024,1024]{1,0:T(8,128)(2,1)} %get-tuple-element.134), channel_id=1, source_target_pairs={{0,2},{1,3},{2,0},{3,1},{4,6},{5,7},{6,4},{7,5}} | collective-permute-start | bytes 6291464 | tf_op jit(solution)/shard_map/ppermute | solution.py:240
  15.8 148.7 %collective-permute-start = (bf16[4096,1024]{1,0:T(8,128)(2,1)}, bf16[4096,1024]{1,0:T(8,128)(2,1)}, u32[]{:S(2)}, u32[]{:S(2)}) collective-permute-start(bf16[4096,1024]{1,0:T(8,128)(2,1)} %constant_dynamic-slice_fusion.9.own_ref), channel_id=1, source_target_pairs={{0,1},{1,0},{2,3},{3,2},{4,5},{5,4},{6,7},{7,6}} | collective-permute-start | bytes 25165832 | tf_op jit(solution)/shard_map/ppermute | solution.py:237
  15.8 83.1 %collective-permute-start.2 = (bf16[1024,1024]{1,0:T(8,128)(2,1)S(1)}, bf16[1024,1024]{1,0:T(8,128)(2,1)}, u32[]{:S(2)}, u32[]{:S(2)}) collective-permute-start(bf16[1024,1024]{1,0:T(8,128)(2,1)S(1)} %copy-done.14), channel_id=1, source_target_pairs={{0,2},{1,3},{2,0},{3,1},{4,6},{5,7},{6,4},{7,5}} | collective-permute-start | bytes 6291464 | tf_op jit(solution)/shard_map/ppermute | solution.py:240
  54.6 46.7 %collective-permute-start.3 = (bf16[1024,1024]{1,0:T(8,128)(2,1)S(1)}, bf16[1024,1024]{1,0:T(8,128)(2,1)}, u32[]{:S(2)}, u32[]{:S(2)}) collective-permute-start(bf16[1024,1024]{1,0:T(8,128)(2,1)S(1)} %collective-permute-done.1.refs_0_), channel_id=1, source_target_pairs={{0,4},{4,0},{1,5},{5,1},{2,6},{6,2},{3,7},{7,3}} | collective-permute-start | bytes 6291464 | tf_op jit(solution)/shard_map/ppermute | solution.py:249
  56.8 44.0 %collective-permute-start.10 = (bf16[4,1024]{1,0:T(4,128)(2,1)S(1)}, bf16[4,1024]{1,0:T(4,128)(2,1)S(1)}, u32[]{:S(2)}, u32[]{:S(2)}) collective-permute-start(bf16[4,1024]{1,0:T(4,128)(2,1)S(1)} %pad_maximum_fusion.1), channel_id=1, source_target_pairs={{0,2},{1,3},{2,0},{3,1},{4,6},{5,7},{6,4},{7,5}} | collective-permute-start | bytes 24584 | tf_op jit(solution)/shard_map/ppermute | solution.py:240
  58.3 42.4 %collective-permute-start.11 = (bf16[4,1024]{1,0:T(4,128)(2,1)S(1)}, bf16[4,1024]{1,0:T(4,128)(2,1)S(1)}, u32[]{:S(2)}, u32[]{:S(2)}) collective-permute-start(bf16[4,1024]{1,0:T(4,128)(2,1)S(1)} %pad_maximum_fusion.1), channel_id=1, source_target_pairs={{0,3},{1,2},{2,1},{3,0},{4,7},{5,6},{6,5},{7,4}} | collective-permute-start | bytes 24584 | tf_op jit(solution)/shard_map/ppermute | solution.py:240
  99.0 46.9 %collective-permute-start.4 = (bf16[1024,1024]{1,0:T(8,128)(2,1)}, bf16[1024,1024]{1,0:T(8,128)(2,1)}, u32[]{:S(2)}, u32[]{:S(2)}) collective-permute-start(bf16[1024,1024]{1,0:T(8,128)(2,1)} %collective-permute-done.2.refs_1_), channel_id=1, source_target_pairs={{0,4},{4,0},{1,5},{5,1},{2,6},{6,2},{3,7},{7,3}} | collective-permute-start | bytes 6291464 | tf_op jit(solution)/shard_map/ppermute | solution.py:249
  100.7 45.2 %collective-permute-start.5 = (bf16[1024,1024]{1,0:T(8,128)(2,1)S(1)}, bf16[1024,1024]{1,0:T(8,128)(2,1)}, u32[]{:S(2)}, u32[]{:S(2)}) collective-permute-start(bf16[1024,1024]{1,0:T(8,128)(2,1)S(1)} %collective-permute-done.1.refs_0_), channel_id=1, source_target_pairs={{0,1},{1,0},{2,3},{3,2},{4,5},{5,4},{6,7},{7,6}} | collective-permute-start | bytes 6291464 | tf_op jit(solution)/shard_map/ppermute | solution.py:237
  100.8 46.6 %collective-permute-start.6 = (bf16[1024,1024]{1,0:T(8,128)(2,1)}, bf16[1024,1024]{1,0:T(8,128)(2,1)}, u32[]{:S(2)}, u32[]{:S(2)}) collective-permute-start(bf16[1024,1024]{1,0:T(8,128)(2,1)} %collective-permute-done.2.refs_1_), channel_id=1, source_target_pairs={{0,1},{1,0},{2,3},{3,2},{4,5},{5,4},{6,7},{7,6}} | collective-permute-start | bytes 6291464 | tf_op jit(solution)/shard_map/ppermute | solution.py:237
  101.3 47.3 %collective-permute-start.7 = (bf16[1024,1024]{1,0:T(8,128)(2,1)}, bf16[1024,1024]{1,0:T(8,128)(2,1)}, u32[]{:S(2)}, u32[]{:S(2)}) collective-permute-start(bf16[1024,1024]{1,0:T(8,128)(2,1)} %collective-permute-done.3.refs_2_), channel_id=1, source_target_pairs={{0,1},{1,0},{2,3},{3,2},{4,5},{5,4},{6,7},{7,6}} | collective-permute-start | bytes 6291464 | tf_op jit(solution)/shard_map/ppermute | solution.py:237
  145.9 50.5 %collective-permute-start.12 = (bf16[1024,1536]{1,0:T(8,128)(2,1)}, bf16[1024,1536]{1,0:T(8,128)(2,1)}, u32[]{:S(2)}, u32[]{:S(2)}) collective-permute-start(bf16[1024,1536]{1,0:T(8,128)(2,1)} %get-tuple-element.145), channel_id=1, source_target_pairs={{0,1},{1,0},{2,3},{3,2},{4,5},{5,4},{6,7},{7,6}} | collective-permute-start | bytes 9437192 | tf_op jit(solution)/shard_map/ppermute | solution.py:237
  145.9 71.3 %collective-permute-start.13 = (bf16[1024,1536]{1,0:T(8,128)(2,1)}, bf16[1024,1536]{1,0:T(8,128)(2,1)}, u32[]{:S(2)}, u32[]{:S(2)}) collective-permute-start(bf16[1024,1536]{1,0:T(8,128)(2,1)} %get-tuple-element.146.refs_0_), channel_id=1, source_target_pairs={{0,2},{1,3},{2,0},{3,1},{4,6},{5,7},{6,4},{7,5}} | collective-permute-start | bytes 9437192 | tf_op jit(solution)/shard_map/ppermute | solution.py:240
  147.4 136.3 %collective-permute-start.14 = (bf16[1024,1536]{1,0:T(8,128)(2,1)}, bf16[1024,1536]{1,0:T(8,128)(2,1)}, u32[]{:S(2)}, u32[]{:S(2)}) collective-permute-start(bf16[1024,1536]{1,0:T(8,128)(2,1)} %get-tuple-element.145), channel_id=1, source_target_pairs={{0,3},{1,2},{2,1},{3,0},{4,7},{5,6},{6,5},{7,4}} | collective-permute-start | bytes 9437192 | tf_op jit(solution)/shard_map/ppermute | solution.py:240
  164.3 268.6 %collective-permute-start.15 = (bf16[1024,1536]{1,0:T(8,128)(2,1)}, bf16[1024,1536]{1,0:T(8,128)(2,1)}, u32[]{:S(2)}, u32[]{:S(2)}) collective-permute-start(bf16[1024,1536]{1,0:T(8,128)(2,1)} %get-tuple-element.143), channel_id=1, source_target_pairs={{0,1},{1,0},{2,3},{3,2},{4,5},{5,4},{6,7},{7,6}} | collective-permute-start | bytes 9437192 | tf_op jit(solution)/shard_map/ppermute | solution.py:237
  164.5 268.4 %collective-permute-start.17 = (bf16[1024,1536]{1,0:T(8,128)(2,1)}, bf16[1024,1536]{1,0:T(8,128)(2,1)}, u32[]{:S(2)}, u32[]{:S(2)}) collective-permute-start(bf16[1024,1536]{1,0:T(8,128)(2,1)} %get-tuple-element.143), channel_id=1, source_target_pairs={{0,3},{1,2},{2,1},{3,0},{4,7},{5,6},{6,5},{7,4}} | collective-permute-start | bytes 9437192 | tf_op jit(solution)/shard_map/ppermute | solution.py:240
  196.4 236.5 %collective-permute-start.16 = (bf16[1024,1536]{1,0:T(8,128)(2,1)}, bf16[1024,1536]{1,0:T(8,128)(2,1)S(1)}, u32[]{:S(2)}, u32[]{:S(2)}) collective-permute-start(bf16[1024,1536]{1,0:T(8,128)(2,1)} %get-tuple-element.68.refs_0_), channel_id=1, source_target_pairs={{0,2},{1,3},{2,0},{3,1},{4,6},{5,7},{6,4},{7,5}} | collective-permute-start | bytes 9437192 | tf_op jit(solution)/shard_map/ppermute | solution.py:240
  472.4 53.7 %collective-permute-start.18 = (bf16[2048,1536]{1,0:T(8,128)(2,1)}, bf16[2048,1536]{1,0:T(8,128)(2,1)}, u32[]{:S(2)}, u32[]{:S(2)}) collective-permute-start(bf16[2048,1536]{1,0:T(8,128)(2,1)} %project.4), channel_id=1, source_target_pairs={{0,1},{1,0},{2,3},{3,2},{4,5},{5,4},{6,7},{7,6}} | collective-permute-start | bytes 18874376 | tf_op jit(solution)/shard_map/ppermute | solution.py:237
  473.5 66.8 %collective-permute-start.20 = (bf16[2816,1024]{1,0:T(8,128)(2,1)}, bf16[2816,1024]{1,0:T(8,128)(2,1)}, u32[]{:S(2)}, u32[]{:S(2)}) collective-permute-start(bf16[2816,1024]{1,0:T(8,128)(2,1)} %param.37), channel_id=1, source_target_pairs={{0,1},{1,0},{2,3},{3,2},{4,5},{5,4},{6,7},{7,6}} | collective-permute-start | bytes 17301512 | tf_op jit(solution)/shard_map/ppermute | solution.py:237
  473.5 127.5 %collective-permute-start.19 = (bf16[2816,1024]{1,0:T(8,128)(2,1)}, bf16[2816,1024]{1,0:T(8,128)(2,1)}, u32[]{:S(2)}, u32[]{:S(2)}) collective-permute-start(bf16[2816,1024]{1,0:T(8,128)(2,1)} %param.37), channel_id=1, source_target_pairs={{0,2},{1,3},{2,0},{3,1},{4,6},{5,7},{6,4},{7,5}} | collective-permute-start | bytes 17301512 | tf_op jit(solution)/shard_map/ppermute | solution.py:240
  480.2 314.6 %collective-permute-start.30 = (bf16[1024,2560]{1,0:T(8,128)(2,1)}, bf16[1024,2560]{1,0:T(8,128)(2,1)}, u32[]{:S(2)}, u32[]{:S(2)}) collective-permute-start(bf16[1024,2560]{1,0:T(8,128)(2,1)} %slice.149.refs_0_), channel_id=1, source_target_pairs={{0,2},{1,3},{2,0},{3,1},{4,6},{5,7},{6,4},{7,5}} | collective-permute-start | bytes 15728648 | tf_op jit(solution)/shard_map/ppermute | solution.py:240
  486.0 339.2 %collective-permute-start.31 = (bf16[1024,2560]{1,0:T(8,128)(2,1)}, bf16[1024,2560]{1,0:T(8,128)(2,1)}, u32[]{:S(2)}, u32[]{:S(2)}) collective-permute-start(bf16[1024,2560]{1,0:T(8,128)(2,1)} %slice.150.refs_4_), channel_id=1, source_target_pairs={{0,2},{1,3},{2,0},{3,1},{4,6},{5,7},{6,4},{7,5}} | collective-permute-start | bytes 15728648 | tf_op jit(solution)/shard_map/ppermute | solution.py:240
  546.3 104.3 %collective-permute-start.27 = (bf16[512,1024]{1,0:T(8,128)(2,1)S(1)}, bf16[512,1024]{1,0:T(8,128)(2,1)S(1)}, u32[]{:S(2)}, u32[]{:S(2)}) collective-permute-start(bf16[512,1024]{1,0:T(8,128)(2,1)S(1)} %fusion.39), channel_id=1, source_target_pairs={{0,4},{4,0},{1,5},{5,1},{2,6},{6,2},{3,7},{7,3}} | collective-permute-start | bytes 3145736 | tf_op jit(solution)/shard_map/ppermute | solution.py:249
  601.0 44.4 %collective-permute-start.21 = (bf16[2816,1024]{1,0:T(8,128)(2,1)}, bf16[2816,1024]{1,0:T(8,128)(2,1)S(1)}, u32[]{:S(2)}, u32[]{:S(2)}) collective-permute-start(bf16[2816,1024]{1,0:T(8,128)(2,1)} %collective-permute-done.19), channel_id=1, source_target_pairs={{0,1},{1,0},{2,3},{3,2},{4,5},{5,4},{6,7},{7,6}} | collective-permute-start | bytes 17301512 | tf_op jit(solution)/shard_map/ppermute | solution.py:237
  606.9 42.2 %collective-permute-start.28 = (bf16[512,1024]{1,0:T(8,128)(2,1)S(1)}, bf16[512,1024]{1,0:T(8,128)(2,1)S(1)}, u32[]{:S(2)}, u32[]{:S(2)}) collective-permute-start(bf16[512,1024]{1,0:T(8,128)(2,1)S(1)} %fusion.30), channel_id=1, source_target_pairs={{0,4},{4,0},{1,5},{5,1},{2,6},{6,2},{3,7},{7,3}} | collective-permute-start | bytes 3145736 | tf_op jit(solution)/shard_map/ppermute | solution.py:249
  649.1 44.8 %collective-permute-start.24 = (bf16[512,1024]{1,0:T(8,128)(2,1)S(1)}, bf16[512,1024]{1,0:T(8,128)(2,1)S(1)}, u32[]{:S(2)}, u32[]{:S(2)}) collective-permute-start(bf16[512,1024]{1,0:T(8,128)(2,1)S(1)} %fusion.24), channel_id=1, source_target_pairs={{0,4},{4,0},{1,5},{5,1},{2,6},{6,2},{3,7},{7,3}} | collective-permute-start | bytes 3145736 | tf_op jit(solution)/shard_map/ppermute | solution.py:249
  650.6 65.9 %collective-permute-start.29 = (bf16[512,1024]{1,0:T(8,128)(2,1)S(1)}, bf16[512,1024]{1,0:T(8,128)(2,1)}, u32[]{:S(2)}, u32[]{:S(2)}) collective-permute-start(bf16[512,1024]{1,0:T(8,128)(2,1)S(1)} %fusion.33), channel_id=1, source_target_pairs={{0,4},{4,0},{1,5},{5,1},{2,6},{6,2},{3,7},{7,3}} | collective-permute-start | bytes 3145736 | tf_op jit(solution)/shard_map/ppermute | solution.py:249
  671.4 67.4 %collective-permute-start.23 = (bf16[512,1024]{1,0:T(8,128)(2,1)}, bf16[512,1024]{1,0:T(8,128)(2,1)S(1)}, u32[]{:S(2)}, u32[]{:S(2)}) collective-permute-start(bf16[512,1024]{1,0:T(8,128)(2,1)} %fusion.21), channel_id=1, source_target_pairs={{0,4},{4,0},{1,5},{5,1},{2,6},{6,2},{3,7},{7,3}} | collective-permute-start | bytes 3145736 | tf_op jit(solution)/shard_map/ppermute | solution.py:249
  693.9 67.4 %collective-permute-start.22 = (bf16[512,1024]{1,0:T(8,128)(2,1)}, bf16[512,1024]{1,0:T(8,128)(2,1)S(1)}, u32[]{:S(2)}, u32[]{:S(2)}) collective-permute-start(bf16[512,1024]{1,0:T(8,128)(2,1)} %fusion.18), channel_id=1, source_target_pairs={{0,4},{4,0},{1,5},{5,1},{2,6},{6,2},{3,7},{7,3}} | collective-permute-start | bytes 3145736 | tf_op jit(solution)/shard_map/ppermute | solution.py:249
  716.4 66.7 %collective-permute-start.25 = (bf16[512,1024]{1,0:T(8,128)(2,1)}, bf16[512,1024]{1,0:T(8,128)(2,1)}, u32[]{:S(2)}, u32[]{:S(2)}) collective-permute-start(bf16[512,1024]{1,0:T(8,128)(2,1)} %fusion.27), channel_id=1, source_target_pairs={{0,4},{4,0},{1,5},{5,1},{2,6},{6,2},{3,7},{7,3}} | collective-permute-start | bytes 3145736 | tf_op jit(solution)/shard_map/ppermute | solution.py:249
  738.8 100.9 %collective-permute-start.34 = (bf16[1024,2560]{1,0:T(8,128)(2,1)}, bf16[1024,2560]{1,0:T(8,128)(2,1)}, u32[]{:S(2)}, u32[]{:S(2)}) collective-permute-start(bf16[1024,2560]{1,0:T(8,128)(2,1)} %slice.149.refs_0_), channel_id=1, source_target_pairs={{0,1},{1,0},{2,3},{3,2},{4,5},{5,4},{6,7},{7,6}} | collective-permute-start | bytes 15728648 | tf_op jit(solution)/shard_map/ppermute | solution.py:237
  761.3 78.4 %collective-permute-start.36 = (bf16[1024,2560]{1,0:T(8,128)(2,1)}, bf16[1024,2560]{1,0:T(8,128)(2,1)}, u32[]{:S(2)}, u32[]{:S(2)}) collective-permute-start(bf16[1024,2560]{1,0:T(8,128)(2,1)} %slice.150.refs_4_), channel_id=1, source_target_pairs={{0,1},{1,0},{2,3},{3,2},{4,5},{5,4},{6,7},{7,6}} | collective-permute-start | bytes 15728648 | tf_op jit(solution)/shard_map/ppermute | solution.py:237
  831.3 64.8 %collective-permute-start.38 = (bf16[1024,1024]{1,0:T(8,128)(2,1)}, bf16[1024,1024]{1,0:T(8,128)(2,1)}, u32[]{:S(2)}, u32[]{:S(2)}) collective-permute-start(bf16[1024,1024]{1,0:T(8,128)(2,1)} %get-tuple-element.139.refs_0_), channel_id=1, source_target_pairs={{0,2},{1,3},{2,0},{3,1},{4,6},{5,7},{6,4},{7,5}} | collective-permute-start | bytes 6291464 | tf_op jit(solution)/shard_map/ppermute | solution.py:240
  839.7 84.4 %collective-permute-start.33 = (bf16[1024,1024]{1,0:T(8,128)(2,1)}, bf16[1024,1024]{1,0:T(8,128)(2,1)}, u32[]{:S(2)}, u32[]{:S(2)}) collective-permute-start(bf16[1024,1024]{1,0:T(8,128)(2,1)} %get-tuple-element.139.refs_0_), channel_id=1, source_target_pairs={{0,1},{1,0},{2,3},{3,2},{4,5},{5,4},{6,7},{7,6}} | collective-permute-start | bytes 6291464 | tf_op jit(solution)/shard_map/ppermute | solution.py:237
  839.7 84.4 %collective-permute-start.39 = (bf16[1024,1024]{1,0:T(8,128)(2,1)}, bf16[1024,1024]{1,0:T(8,128)(2,1)}, u32[]{:S(2)}, u32[]{:S(2)}) collective-permute-start(bf16[1024,1024]{1,0:T(8,128)(2,1)} %get-tuple-element.137.refs_4_), channel_id=1, source_target_pairs={{0,2},{1,3},{2,0},{3,1},{4,6},{5,7},{6,4},{7,5}} | collective-permute-start | bytes 6291464 | tf_op jit(solution)/shard_map/ppermute | solution.py:240
  840.5 119.8 %collective-permute-start.44 = (bf16[512,4096]{1,0:T(8,128)(2,1)}, bf16[512,4096]{1,0:T(8,128)(2,1)}, u32[]{:S(2)}, u32[]{:S(2)}) collective-permute-start(bf16[512,4096]{1,0:T(8,128)(2,1)} %get-tuple-element.86.high_ref), channel_id=1, source_target_pairs={{0,4},{4,0},{1,5},{5,1},{2,6},{6,2},{3,7},{7,3}} | collective-permute-start | bytes 12582920 | tf_op jit(solution)/shard_map/ppermute | solution.py:249
  842.1 181.3 %collective-permute-start.43 = (bf16[512,4096]{1,0:T(8,128)(2,1)}, bf16[512,4096]{1,0:T(8,128)(2,1)}, u32[]{:S(2)}, u32[]{:S(2)}) collective-permute-start(bf16[512,4096]{1,0:T(8,128)(2,1)} %get-tuple-element.85.low_ref), channel_id=1, source_target_pairs={{0,4},{4,0},{1,5},{5,1},{2,6},{6,2},{3,7},{7,3}} | collective-permute-start | bytes 12582920 | tf_op jit(solution)/shard_map/ppermute | solution.py:249
  925.9 177.0 %collective-permute-start.45 = (bf16[1024,1024]{1,0:T(8,128)(2,1)S(1)}, bf16[1024,1024]{1,0:T(8,128)(2,1)}, u32[]{:S(2)}, u32[]{:S(2)}) collective-permute-start(bf16[1024,1024]{1,0:T(8,128)(2,1)S(1)} %get-tuple-element.140.refs_0_), channel_id=1, source_target_pairs={{0,2},{1,3},{2,0},{3,1},{4,6},{5,7},{6,4},{7,5}} | collective-permute-start | bytes 6291464 | tf_op jit(solution)/shard_map/ppermute | solution.py:240
  928.5 177.3 %collective-permute-start.47 = (bf16[1024,1024]{1,0:T(8,128)(2,1)S(1)}, bf16[1024,1024]{1,0:T(8,128)(2,1)}, u32[]{:S(2)}, u32[]{:S(2)}) collective-permute-start(bf16[1024,1024]{1,0:T(8,128)(2,1)S(1)} %get-tuple-element.140.refs_0_), channel_id=1, source_target_pairs={{0,1},{1,0},{2,3},{3,2},{4,5},{5,4},{6,7},{7,6}} | collective-permute-start | bytes 6291464 | tf_op jit(solution)/shard_map/ppermute | solution.py:237
  932.8 170.0 %collective-permute-start.46 = (bf16[1024,1024]{1,0:T(8,128)(2,1)}, bf16[1024,1024]{1,0:T(8,128)(2,1)}, u32[]{:S(2)}, u32[]{:S(2)}) collective-permute-start(bf16[1024,1024]{1,0:T(8,128)(2,1)} %get-tuple-element.136.refs_4_), channel_id=1, source_target_pairs={{0,2},{1,3},{2,0},{3,1},{4,6},{5,7},{6,4},{7,5}} | collective-permute-start | bytes 6291464 | tf_op jit(solution)/shard_map/ppermute | solution.py:240
  960.3 145.5 %collective-permute-start.49 = (bf16[1024,1024]{1,0:T(8,128)(2,1)}, bf16[1024,1024]{1,0:T(8,128)(2,1)}, u32[]{:S(2)}, u32[]{:S(2)}) collective-permute-start(bf16[1024,1024]{1,0:T(8,128)(2,1)} %get-tuple-element.136.refs_4_), channel_id=1, source_target_pairs={{0,1},{1,0},{2,3},{3,2},{4,5},{5,4},{6,7},{7,6}} | collective-permute-start | bytes 6291464 | tf_op jit(solution)/shard_map/ppermute | solution.py:237
  1103.4 59.0 %collective-permute-start.51 = (bf16[1024,1024]{1,0:T(8,128)(2,1)}, bf16[1024,1024]{1,0:T(8,128)(2,1)}, u32[]{:S(2)}, u32[]{:S(2)}) collective-permute-start(bf16[1024,1024]{1,0:T(8,128)(2,1)} %get-tuple-element.138.refs_0_), channel_id=1, source_target_pairs={{0,2},{1,3},{2,0},{3,1},{4,6},{5,7},{6,4},{7,5}} | collective-permute-start | bytes 6291464 | tf_op jit(solution)/shard_map/ppermute | solution.py:240
  1105.8 95.1 %collective-permute-start.53 = (bf16[1024,1024]{1,0:T(8,128)(2,1)}, bf16[1024,1024]{1,0:T(8,128)(2,1)}, u32[]{:S(2)}, u32[]{:S(2)}) collective-permute-start(bf16[1024,1024]{1,0:T(8,128)(2,1)} %get-tuple-element.138.refs_0_), channel_id=1, source_target_pairs={{0,1},{1,0},{2,3},{3,2},{4,5},{5,4},{6,7},{7,6}} | collective-permute-start | bytes 6291464 | tf_op jit(solution)/shard_map/ppermute | solution.py:237
  1105.8 90.4 %collective-permute-start.52 = (bf16[1024,1024]{1,0:T(8,128)(2,1)}, bf16[1024,1024]{1,0:T(8,128)(2,1)}, u32[]{:S(2)}, u32[]{:S(2)}) collective-permute-start(bf16[1024,1024]{1,0:T(8,128)(2,1)} %get-tuple-element.135.refs_4_), channel_id=1, source_target_pairs={{0,2},{1,3},{2,0},{3,1},{4,6},{5,7},{6,4},{7,5}} | collective-permute-start | bytes 6291464 | tf_op jit(solution)/shard_map/ppermute | solution.py:240
  1107.4 94.8 %collective-permute-start.55 = (bf16[1024,1024]{1,0:T(8,128)(2,1)}, bf16[1024,1024]{1,0:T(8,128)(2,1)}, u32[]{:S(2)}, u32[]{:S(2)}) collective-permute-start(bf16[1024,1024]{1,0:T(8,128)(2,1)} %get-tuple-element.135.refs_4_), channel_id=1, source_target_pairs={{0,1},{1,0},{2,3},{3,2},{4,5},{5,4},{6,7},{7,6}} | collective-permute-start | bytes 6291464 | tf_op jit(solution)/shard_map/ppermute | solution.py:237
  1110.4 194.0 %collective-permute-start.62 = (bf16[6144,1024]{1,0:T(8,128)(2,1)}, bf16[6144,1024]{1,0:T(8,128)(2,1)}, u32[]{:S(2)}, u32[]{:S(2)}) collective-permute-start(bf16[6144,1024]{1,0:T(8,128)(2,1)} %param.44), channel_id=1, source_target_pairs={{0,1},{1,0},{2,3},{3,2},{4,5},{5,4},{6,7},{7,6}} | collective-permute-start | bytes 37748744 | tf_op jit(solution)/shard_map/ppermute | solution.py:237
  1201.0 56.9 %collective-permute-start.57 = (bf16[1024,512]{1,0:T(8,128)(2,1)S(1)}, bf16[1024,512]{1,0:T(8,128)(2,1)S(1)}, u32[]{:S(2)}, u32[]{:S(2)}) collective-permute-start(bf16[1024,512]{1,0:T(8,128)(2,1)S(1)} %slice.151.refs_0_), channel_id=1, source_target_pairs={{0,2},{1,3},{2,0},{3,1},{4,6},{5,7},{6,4},{7,5}} | collective-permute-start | bytes 3145736 | tf_op jit(solution)/shard_map/ppermute | solution.py:240
  1202.2 65.2 %collective-permute-start.32 = (bf16[1024,512]{1,0:T(8,128)(2,1)S(1)}, bf16[1024,512]{1,0:T(8,128)(2,1)}, u32[]{:S(2)}, u32[]{:S(2)}) collective-permute-start(bf16[1024,512]{1,0:T(8,128)(2,1)S(1)} %slice.151.refs_0_), channel_id=1, source_target_pairs={{0,1},{1,0},{2,3},{3,2},{4,5},{5,4},{6,7},{7,6}} | collective-permute-start | bytes 3145736 | tf_op jit(solution)/shard_map/ppermute | solution.py:237
  1202.2 55.6 %collective-permute-start.58 = (bf16[1024,512]{1,0:T(8,128)(2,1)S(1)}, bf16[1024,512]{1,0:T(8,128)(2,1)}, u32[]{:S(2)}, u32[]{:S(2)}) collective-permute-start(bf16[1024,512]{1,0:T(8,128)(2,1)S(1)} %slice.166.refs_4_), channel_id=1, source_target_pairs={{0,2},{1,3},{2,0},{3,1},{4,6},{5,7},{6,4},{7,5}} | collective-permute-start | bytes 3145736 | tf_op jit(solution)/shard_map/ppermute | solution.py:240
  1205.0 63.3 %collective-permute-start.60 = (bf16[1024,512]{1,0:T(8,128)(2,1)S(1)}, bf16[1024,512]{1,0:T(8,128)(2,1)}, u32[]{:S(2)}, u32[]{:S(2)}) collective-permute-start(bf16[1024,512]{1,0:T(8,128)(2,1)S(1)} %slice.166.refs_4_), channel_id=1, source_target_pairs={{0,1},{1,0},{2,3},{3,2},{4,5},{5,4},{6,7},{7,6}} | collective-permute-start | bytes 3145736 | tf_op jit(solution)/shard_map/ppermute | solution.py:237
  1267.5 205.2 %collective-permute-start.68 = (bf16[6144,768]{1,0:T(8,128)(2,1)}, bf16[6144,768]{1,0:T(8,128)(2,1)}, u32[]{:S(2)}, u32[]{:S(2)}) collective-permute-start(bf16[6144,768]{1,0:T(8,128)(2,1)} %slice.171), channel_id=1, source_target_pairs={{0,2},{1,3},{2,0},{3,1},{4,6},{5,7},{6,4},{7,5}} | collective-permute-start | bytes 28311560 | tf_op jit(solution)/shard_map/ppermute | solution.py:240
  1302.9 70.0 %collective-permute-start.66 = (bf16[1024,1024]{1,0:T(8,128)(2,1)}, bf16[1024,1024]{1,0:T(8,128)(2,1)}, u32[]{:S(2)}, u32[]{:S(2)}) collective-permute-start(bf16[1024,1024]{1,0:T(8,128)(2,1)} %convolution_convert_fusion.1), channel_id=1, source_target_pairs={{0,4},{4,0},{1,5},{5,1},{2,6},{6,2},{3,7},{7,3}} | collective-permute-start | bytes 6291464 | tf_op jit(solution)/shard_map/ppermute | solution.py:249
  1321.1 74.5 %collective-permute-start.63 = (bf16[1024,1024]{1,0:T(8,128)(2,1)}, bf16[1024,1024]{1,0:T(8,128)(2,1)S(1)}, u32[]{:S(2)}, u32[]{:S(2)}) collective-permute-start(bf16[1024,1024]{1,0:T(8,128)(2,1)} %convolution_convert_fusion), channel_id=1, source_target_pairs={{0,4},{4,0},{1,5},{5,1},{2,6},{6,2},{3,7},{7,3}} | collective-permute-start | bytes 6291464 | tf_op jit(solution)/shard_map/ppermute | solution.py:249
  1474.8 70.6 %collective-permute-start.70 = (bf16[6144,256]{1,0:T(8,128)(2,1)S(1)}, bf16[6144,256]{1,0:T(8,128)(2,1)}, u32[]{:S(2)}, u32[]{:S(2)}) collective-permute-start(bf16[6144,256]{1,0:T(8,128)(2,1)S(1)} %slice.172), channel_id=1, source_target_pairs={{0,2},{1,3},{2,0},{3,1},{4,6},{5,7},{6,4},{7,5}} | collective-permute-start | bytes 9437192 | tf_op jit(solution)/shard_map/ppermute | solution.py:240
  1476.0 71.4 %collective-permute-start.64 = (bf16[1024,1024]{1,0:T(8,128)(2,1)}, bf16[1024,1024]{1,0:T(8,128)(2,1)}, u32[]{:S(2)}, u32[]{:S(2)}) collective-permute-start(bf16[1024,1024]{1,0:T(8,128)(2,1)} %add_convert_fusion.1), channel_id=1, source_target_pairs={{0,1},{1,0},{2,3},{3,2},{4,5},{5,4},{6,7},{7,6}} | collective-permute-start | bytes 6291464 | tf_op jit(solution)/shard_map/ppermute | solution.py:237
  1491.1 43.0 %collective-permute-start.71 = (bf16[1024,768]{1,0:T(8,128)(2,1)S(1)}, bf16[1024,768]{1,0:T(8,128)(2,1)S(1)}, u32[]{:S(2)}, u32[]{:S(2)}) collective-permute-start(bf16[1024,768]{1,0:T(8,128)(2,1)S(1)} %convolution_convert_fusion.3), channel_id=1, source_target_pairs={{0,4},{4,0},{1,5},{5,1},{2,6},{6,2},{3,7},{7,3}} | collective-permute-start | bytes 4718600 | tf_op jit(solution)/shard_map/ppermute | solution.py:249
  1545.4 44.0 %collective-permute-start.72 = (bf16[6144,256]{1,0:T(8,128)(2,1)}, bf16[6144,256]{1,0:T(8,128)(2,1)}, u32[]{:S(2)}, u32[]{:S(2)}) collective-permute-start(bf16[6144,256]{1,0:T(8,128)(2,1)} %collective-permute-done.70), channel_id=1, source_target_pairs={{0,1},{1,0},{2,3},{3,2},{4,5},{5,4},{6,7},{7,6}} | collective-permute-start | bytes 9437192 | tf_op jit(solution)/shard_map/ppermute | solution.py:237
  1545.4 37.5 %collective-permute-start.75 = (bf16[1024,768]{1,0:T(8,128)(2,1)}, bf16[1024,768]{1,0:T(8,128)(2,1)S(1)}, u32[]{:S(2)}, u32[]{:S(2)}) collective-permute-start(bf16[1024,768]{1,0:T(8,128)(2,1)} %convolution_convert_fusion.2), channel_id=1, source_target_pairs={{0,4},{4,0},{1,5},{5,1},{2,6},{6,2},{3,7},{7,3}} | collective-permute-start | bytes 4718600 | tf_op jit(solution)/shard_map/ppermute | solution.py:249
  1546.9 140.7 %collective-permute-start.67 = (bf16[1024,1024]{1,0:T(8,128)(2,1)}, bf16[1024,1024]{1,0:T(8,128)(2,1)}, u32[]{:S(2)}, u32[]{:S(2)}) collective-permute-start(bf16[1024,1024]{1,0:T(8,128)(2,1)} %add_convert_fusion), channel_id=1, source_target_pairs={{0,4},{4,0},{1,5},{5,1},{2,6},{6,2},{3,7},{7,3}} | collective-permute-start | bytes 6291464 | tf_op jit(solution)/shard_map/ppermute | solution.py:249
  1547.4 141.4 %collective-permute-start.65 = (bf16[1024,1024]{1,0:T(8,128)(2,1)}, bf16[1024,1024]{1,0:T(8,128)(2,1)}, u32[]{:S(2)}, u32[]{:S(2)}) collective-permute-start(bf16[1024,1024]{1,0:T(8,128)(2,1)} %collective-permute-done.64), channel_id=1, source_target_pairs={{0,4},{4,0},{1,5},{5,1},{2,6},{6,2},{3,7},{7,3}} | collective-permute-start | bytes 6291464 | tf_op jit(solution)/shard_map/ppermute | solution.py:249
  1582.9 101.2 %collective-permute-start.78 = (bf16[1024,256]{1,0:T(8,128)(2,1)}, bf16[1024,256]{1,0:T(8,128)(2,1)}, u32[]{:S(2)}, u32[]{:S(2)}) collective-permute-start(bf16[1024,256]{1,0:T(8,128)(2,1)} %convolution_convert_fusion.5), channel_id=1, source_target_pairs={{0,4},{4,0},{1,5},{5,1},{2,6},{6,2},{3,7},{7,3}} | collective-permute-start | bytes 1572872 | tf_op jit(solution)/shard_map/ppermute | solution.py:249
  1589.4 178.5 %collective-permute-start.74 = (bf16[1024,768]{1,0:T(8,128)(2,1)}, bf16[1024,768]{1,0:T(8,128)(2,1)}, u32[]{:S(2)}, u32[]{:S(2)}) collective-permute-start(bf16[1024,768]{1,0:T(8,128)(2,1)} %collective-permute-done.73), channel_id=1, source_target_pairs={{0,4},{4,0},{1,5},{5,1},{2,6},{6,2},{3,7},{7,3}} | collective-permute-start | bytes 4718600 | tf_op jit(solution)/shard_map/ppermute | solution.py:249
  1626.1 152.0 %collective-permute-start.77 = (bf16[1024,768]{1,0:T(8,128)(2,1)S(1)}, bf16[1024,768]{1,0:T(8,128)(2,1)}, u32[]{:S(2)}, u32[]{:S(2)}) collective-permute-start(bf16[1024,768]{1,0:T(8,128)(2,1)S(1)} %collective-permute-done.76), channel_id=1, source_target_pairs={{0,4},{4,0},{1,5},{5,1},{2,6},{6,2},{3,7},{7,3}} | collective-permute-start | bytes 4718600 | tf_op jit(solution)/shard_map/ppermute | solution.py:249
  1684.1 78.1 %collective-permute-start.81 = (bf16[1024,256]{1,0:T(8,128)(2,1)}, bf16[1024,256]{1,0:T(8,128)(2,1)S(1)}, u32[]{:S(2)}, u32[]{:S(2)}) collective-permute-start(bf16[1024,256]{1,0:T(8,128)(2,1)} %convolution_convert_fusion.4), channel_id=1, source_target_pairs={{0,4},{4,0},{1,5},{5,1},{2,6},{6,2},{3,7},{7,3}} | collective-permute-start | bytes 1572872 | tf_op jit(solution)/shard_map/ppermute | solution.py:249
  1687.6 78.8 %collective-permute-start.79 = (bf16[1024,256]{1,0:T(8,128)(2,1)S(1)}, bf16[1024,256]{1,0:T(8,128)(2,1)S(1)}, u32[]{:S(2)}, u32[]{:S(2)}) collective-permute-start(bf16[1024,256]{1,0:T(8,128)(2,1)S(1)} %add_convert_fusion.5), channel_id=1, source_target_pairs={{0,2},{1,3},{2,0},{3,1},{4,6},{5,7},{6,4},{7,5}} | collective-permute-start | bytes 1572872 | tf_op jit(solution)/shard_map/ppermute | solution.py:240
  (76 other events, 2136.2 us)
